TPU v7x, 512 devices: a 4x2x32 block of a 4x8x32 slice. The times are simulated.
512 devices in a mesh: grp: 2 (over y), row: 32 (over z), col: 4 (over x), sub: 2 (over core).
Axes of the slice: x: 4, y: 2, z: 32, core: 2. Of those that a mesh axis runs over, the one named last changes fastest.
The devices are a block of a 4x8x32 slice.
Arguments:
- pair: bfloat16 [768, 384, 128], P(('grp', 'row'), 'col'), parts along dimension 0, may hold values from -6 to 6
- length: int32 [2], P('grp'), parts along dimension 0, may hold values from 192 to 384
- chain: int32 [768], P('grp'), parts along dimension 0, may hold values from 0 to 3, never falling along the last dimension, each value on 1 to 192 neighbouring positions
- att_proj: bfloat16 [128, 4, 128], P(None, None, 'sub'), may hold values from -0.5 to 0.5
- att_bias: bfloat16 [128, 4], P(None, 'sub')
- chain_bias: float32 [4], P('sub'), may hold values from -2 to 2
- att_out: bfloat16 [128, 128], P('sub'), may hold values from -0.5 to 0.5
- mult_in: bfloat16 [128, 512], replicated, may hold values from -0.5 to 0.5
- mult_gate: bfloat16 [128, 128], replicated, may hold values from -0.5 to 0.5
- mult_out: bfloat16 [128, 128], replicated, may hold values from -0.5 to 0.5
- trans_up: bfloat16 [128, 512], replicated, may hold values from -0.5 to 0.5
- trans_down: bfloat16 [512, 128], replicated, may hold values from -0.25 to 0.25
Outputs:
- pair_out: bfloat16 [768, 384, 128], P(('grp', 'row'), ('col', 'sub')), parts along dimension 0
There are 2 independent parts, one for each index of `grp`. A program takes and returns all parts, laid end to end along the dimension named above; an argument that names none is the same for every part. Nothing has to cross between parts.
Inputs may be any that keep to these rules, and one draw needn't show every extreme that they name: chain numbers never fall along the residues; each chain has 1 to 192 residues.
All inputs are finite; a program needn't handle non-finite values.
Results may differ from a plain program's by a relative error of at most 0.012.
The roundings to bfloat16 on the way count: a program that leaves them out, or rounds other values in their place, can miss the bound.
Values may be sent and summed in bfloat16 or wider, within the bound.
A program may use at most 64 MiB of HBM per device.

v0:
```python
import jax
import jax.numpy as jnp
from jax import lax
from jax.sharding import PartitionSpec as P


def sent_together(arrays, axis, dim, along):
    ends, at = ([], 0)
    for a in arrays[:-1]:
        at += a.shape[along]
        ends.append(at)
    both = jnp.concatenate(arrays, axis=along)
    return tuple(jnp.split(lax.all_gather(both, axis, axis=dim, tiled=True), ends, axis=along))


def joined_along(blocks, dim):
    shape = list(blocks.shape[1:])
    shape[dim] *= blocks.shape[0]
    return jnp.moveaxis(blocks, 0, dim).reshape(shape)


def copy_for_each(shard, axis):
    devices = lax.axis_size(axis)
    return lax.all_to_all(
        jnp.broadcast_to(shard[None], (devices, *shard.shape)), axis, 0, 0, tiled=True
    )


def collect(shard, axis, dim):
    return joined_along(copy_for_each(shard, axis), dim)


def cut_along(shard, dim, devices):
    before, after = (shard.shape[:dim], shard.shape[dim + 1 :])
    return jnp.moveaxis(shard.reshape(*before, devices, -1, *after), dim, 0)


def sum_at_owner(shard, axis, dim):
    devices = lax.axis_size(axis)
    blocks = lax.all_to_all(cut_along(shard, dim, devices), axis, 0, 0, tiled=True)
    return jnp.sum(blocks.astype(jnp.float32), axis=0)


def norm(value):
    mean = jnp.mean(value, axis=-1, keepdims=True)
    centred = value - mean
    variance = jnp.mean(centred * centred, axis=-1, keepdims=True)
    return centred * lax.rsqrt(variance + 1e-05)


def local(
    pair,
    length,
    chain,
    att_proj,
    att_bias,
    chain_bias,
    att_out,
    mult_in,
    mult_gate,
    mult_out,
    trans_up,
    trans_down,
):
    rows, cols, width = pair.shape
    row_count = lax.axis_size("row")
    sub_count = lax.axis_size("sub")
    row_index = lax.axis_index("row")
    col_index = lax.axis_index("col")
    sub_index = lax.axis_index("sub")
    total = rows * row_count
    half = cols // sub_count
    heads_here = att_bias.shape[1]
    spread = att_out.shape[0]
    head_dim = spread // heads_here
    mult_width = mult_out.shape[0]
    valid = (jnp.arange(total) < length[0]).astype(jnp.float32)
    normed = norm(pair.astype(jnp.float32)).astype(jnp.bfloat16)
    flat = normed.reshape(rows * cols, width)
    projected = jnp.dot(
        flat, att_proj.reshape(width, 4 * spread), preferred_element_type=jnp.float32
    ).reshape(rows, cols, 4, spread)
    query = (projected[:, :, 0] * head_dim ** (-0.5)).astype(jnp.bfloat16)
    keys = projected[:, :, 1].astype(jnp.bfloat16)
    values = projected[:, :, 2].astype(jnp.bfloat16)
    gating = jax.nn.sigmoid(projected[:, :, 3])
    bias_local = (
        jnp.dot(flat, att_bias, preferred_element_type=jnp.float32)
        .reshape(rows, cols, heads_here)
        .transpose(2, 0, 1)
    )
    keys_all, values_all = sent_together((keys, values), "col", 1, 0)
    column_bias = collect(bias_local, "row", 1)
    bias_here = lax.all_to_all(column_bias, "col", split_axis=1, concat_axis=2, tiled=True)
    chain_here = lax.dynamic_slice_in_dim(chain, col_index * cols, cols, 0)
    same = (chain_here[:, None] == chain[None, :]).astype(jnp.float32)
    bias_here = (
        bias_here
        + chain_bias[:, None, None] * same[None]
        + (valid[None, None, :] - 1.0) * 1000000000.0
    )

    def attend(block):
        block_query, block_keys, block_values = block
        scores = (
            jnp.einsum(
                "ajhd,akhd->ahjk", block_query, block_keys, preferred_element_type=jnp.float32
            )
            + bias_here[None]
        )
        weights = jax.nn.softmax(scores, axis=-1).astype(jnp.bfloat16)
        return jnp.einsum(
            "ahjk,akhd->ajhd", weights, block_values, preferred_element_type=jnp.float32
        )

    attended = lax.map(
        attend,
        (
            query.reshape(rows // 2, 2, cols, heads_here, head_dim),
            keys_all.reshape(rows // 2, 2, total, heads_here, head_dim),
            values_all.reshape(rows // 2, 2, total, heads_here, head_dim),
        ),
    )
    attended = (attended.reshape(rows, cols, spread) * gating).astype(jnp.bfloat16)
    update = jnp.dot(
        attended.reshape(rows * cols, spread), att_out, preferred_element_type=jnp.float32
    ).reshape(rows, cols, width)
    update_half = sum_at_owner(update.astype(jnp.bfloat16), "sub", 1)
    pair_half = lax.dynamic_slice_in_dim(pair, sub_index * half, half, 1).astype(jnp.float32)
    first = pair_half + update_half
    mixed = norm(first).astype(jnp.bfloat16)
    mixed_flat = mixed.reshape(rows * half, width)
    quad = jnp.dot(mixed_flat, mult_in, preferred_element_type=jnp.float32).reshape(
        rows, half, 4, mult_width
    )
    row_valid = lax.dynamic_slice_in_dim(valid, row_index * rows, rows, 0)
    col_valid = lax.dynamic_slice_in_dim(valid, col_index * cols + sub_index * half, half, 0)
    outer = row_valid[:, None, None] * col_valid[None, :, None]
    left = (outer * jax.nn.sigmoid(quad[:, :, 1]) * quad[:, :, 0]).astype(jnp.bfloat16)
    right = (outer * jax.nn.sigmoid(quad[:, :, 3]) * quad[:, :, 2]).astype(jnp.bfloat16)
    gate_out = jax.nn.sigmoid(jnp.dot(mixed_flat, mult_gate, preferred_element_type=jnp.float32))
    partial_value = jnp.einsum(
        "ikc,jkc->ijc",
        left,
        lax.all_gather(right, "row", axis=0, tiled=True),
        preferred_element_type=jnp.float32,
    )
    tri = sum_at_owner(partial_value.astype(jnp.bfloat16), ("col", "sub"), 1)
    tri_normed = norm(tri).astype(jnp.bfloat16).reshape(rows * half, mult_width)
    second = first + (
        gate_out * jnp.dot(tri_normed, mult_out, preferred_element_type=jnp.float32)
    ).reshape(rows, half, width)
    last_normed = norm(second).astype(jnp.bfloat16).reshape(rows * half, width)
    hidden = jax.nn.relu(jnp.dot(last_normed, trans_up, preferred_element_type=jnp.float32)).astype(
        jnp.bfloat16
    )
    result = second + jnp.dot(hidden, trans_down, preferred_element_type=jnp.float32).reshape(
        rows, half, width
    )
    return result.astype(jnp.bfloat16)


def solution(mesh):
    placed = (
        P(("grp", "row"), "col", None),
        P("grp"),
        P("grp"),
        P(None, None, "sub"),
        P(None, "sub"),
        P("sub"),
        P("sub", None),
        P(),
        P(),
        P(),
        P(),
        P(),
    )
    return jax.shard_map(
        local,
        mesh=mesh,
        in_specs=placed,
        out_specs=P(("grp", "row"), ("col", "sub"), None),
        check_vma=False,
    )
```

profile of v0, /device:TPU:33, one launch (start us, length us, event | category | flops | bytes accessed | tf_op | source)
XLA Modules:
  0.0 350.1 jit_solution(3556476479673316180)
XLA Ops:
  6.6 1.2 convert_reduce_fusion.2
  7.8 1.4 fusion.28
  9.2 1.4 convolution_bitcast_fusion.1
  10.7 0.9 broadcast_in_dim.8
  11.5 46.3 %all-to-all-start = ((f32[32,2,12,96]{3,1,2,0:T(2,128)}), f32[32,2,12,96]{3,1,2,0:T(2,128)}, u32[]{:S(2)}, u32[]{:S(2)}) async-start(f32[32,2,12,96]{3,1,2,0:T(2,128)} %broadcast_in_dim.8), calls=%async_computation | async-start | bytes 786432 | tf_op jit(solution)/shard_map/all_to_all | solution.py:24
  58.0 0.9 fusion.79
  59.0 1.2 copy.71
  61.5 47.7 %all-to-all-done = f32[32,2,12,96]{3,1,2,0:T(2,128)} async-done(((f32[32,2,12,96]{3,1,2,0:T(2,128)}), f32[32,2,12,96]{3,1,2,0:T(2,128)}, u32[]{:S(2)}, u32[]{:S(2)}) %all-to-all-start) | async-done | bytes 294944 | tf_op jit(solution)/shard_map/all_to_all | solution.py:24
  109.2 4.3 %all-to-all-start.1 = ((f32[2,384,96]{2,0,1:T(2,128)}), f32[2,384,96]{2,0,1:T(2,128)S(1)}, u32[]{:S(2)}, u32[]{:S(2)}) async-start(f32[2,384,96]{2,0,1:T(2,128)} %bitcast.19), calls=%async_computation.1 | async-start | bytes 786432 | tf_op jit(solution)/shard_map/all_to_all | solution.py:94
  113.5 3.7 %fusion.78 = (bf16[12,384,64]{2,0,1:T(8,128)(2,1)S(1)}, bf16[12,384,64]{2,0,1:T(8,128)(2,1)}) fusion(bf16[24,384,64]{2,0,1:T(8,128)(2,1)} %all-gather.3.cloned.1.call-done), kind=kLoop, calls=%fused_computation.111 | loop fusion | bytes 2359296 | tf_op jit(solution)/shard_map/split | solution.py:13
  117.3 2.6 copy.91
  119.9 1.5 copy.92
  122.4 14.8 %while.10 = (s32[]{:T(128)}, f32[6,2,96,2,32]{2,4,3,1,0:T(8,128)S(1)}, bf16[6,2,384,2,32]{2,4,3,1,0:T(8,128)(2,1)}, bf16[6,2,96,2,32]{2,4,3,1,0:T(8,128)(2,1)S(1...) while((s32[]{:T(128)}, f32[6,2,96,2,32]{2,4,3,1,0:T(8,128)S(1)}, ...), condition=%wide.region_5.6_spmd, body=%wide.region_2.5_spmd.sunk | while | flops 29344896 | bytes 2792013 | solution.py:116
  122.7 0.5 fusion.105
  123.2 1.7 fusion.106
  125.6 1.7 fusion.106
  128.1 1.7 fusion.106
  130.6 1.7 fusion.106
  133.0 1.7 fusion.106
  135.5 1.7 fusion.106
  137.2 1.3 convolution_convert_fusion.1
  138.6 6.7 %all_to_all.33 = bf16[2,12,48,128]{3,2,1,0:T(8,128)(2,1)S(1)} all-to-all(bf16[2,12,48,128]{3,2,1,0:T(8,128)(2,1)S(1)} %bitcast.193), channel_id=1, replica_groups=mesh['grp'=2,'row'=32,'col'=4,'sub'=2] {'sub'}, dimensions={0} | all-to-all | bytes 589824 | tf_op jit(solution)/shard_map/all_to_all | solution.py:40
  146.0 0.7 copy-done.3
  147.0 0.8 fusion.39
  148.3 121.5 %all-gather.5.cloned.1.call-done = bf16[384,48,128]{2,1,0:T(8,128)(2,1)} async-done(((bf16[12,48,128]{2,1,0:T(8,128)(2,1)}), bf16[384,48,128]{2,1,0:T(8,128)(2,1)}) %all-gather.5.cloned.1.call-update) | async-done | bytes 4718608 | tf_op jit(solution)/shard_map/all_gather | solution.py:145
  269.9 17.9 %copy.81 = bf16[384,48,128]{1,0,2:T(8,128)(2,1)} copy(bf16[384,48,128]{2,1,0:T(8,128)(2,1)} %all-gather.5.cloned.1.call-done) | data formatting | bytes 9437184 | tf_op jit(solution)/shard_map/all_gather | solution.py:145
  287.8 9.0 %fusion.20 = bf16[12,384,128]{1,0,2:T(8,128)(2,1)S(1)} fusion(bf16[384,48,128]{1,0,2:T(8,128)(2,1)} %copy.81, bf16[12,48,128]{1,0,2:T(8,128)(2,1)S(1)} %copy.82), kind=kOutput, calls=%fused_computation.21 | convolution fusion | flops 57212928 | bytes 6045696 | tf_op jit(solution)/shard_map/ikc,jkc->ijc/dot_general | solution.py:142
  296.8 1.3 copy.83
  298.1 1.1 copy.84
  299.2 24.6 %all-to-all-start.3 = ((bf16[8,12,48,128]{3,2,1,0:T(8,128)(2,1)}), bf16[8,12,48,128]{3,2,1,0:T(8,128)(2,1)S(1)}, u32[]{:S(2)}, u32[]{:S(2)}) async-start(bf16[8,12,48,128]{3,2,1,0:T(8,128)(2,1)} %copy.84), calls=%async_computation.3 | async-start | bytes 2359296 | tf_op jit(solution)/shard_map/all_to_all | solution.py:40
  324.1 16.1 %all-to-all-done.3 = bf16[8,12,48,128]{3,2,1,0:T(8,128)(2,1)S(1)} async-done(((bf16[8,12,48,128]{3,2,1,0:T(8,128)(2,1)}), bf16[8,12,48,128]{3,2,1,0:T(8,128)(2,1)S(1)}, u32[]{:S(2)}, u32[]{:S(2)}) %all-to-all-start.3) | async-done | bytes 1179680 | tf_op jit(solution)/shard_map/all_to_all | solution.py:40
  342.5 0.7 add_convert_fusion
  (85 shorter events, 9.9 us)
Async XLA Ops:
  6.5 335.5 %copy-start = (bf16[512,128]{1,0:T(8,128)(2,1)S(1)}, bf16[512,128]{1,0:T(8,128)(2,1)}, u32[]{:S(2)}) copy-start(bf16[512,128]{1,0:T(8,128)(2,1)} %param.25) | copy-start | bytes 393220
  6.6 51.4 %copy-start.1 = (bf16[12,96,128]{2,1,0:T(8,128)(2,1)S(1)}, bf16[12,96,128]{2,1,0:T(8,128)(2,1)}, u32[]{:S(2)}) copy-start(bf16[12,96,128]{2,1,0:T(8,128)(2,1)} %param.14) | copy-start | bytes 884740
  6.6 51.4 %copy-start.6 = (bf16[128,4,64]{0,2,1:T(8,128)(2,1)S(1)}, bf16[128,4,64]{0,2,1:T(8,128)(2,1)}, u32[]{:S(2)}) copy-start(bf16[128,4,64]{0,2,1:T(8,128)(2,1)} %param.17) | copy-start | bytes 196612
  11.5 97.7 %all-to-all-start = ((f32[32,2,12,96]{3,1,2,0:T(2,128)}), f32[32,2,12,96]{3,1,2,0:T(2,128)}, u32[]{:S(2)}, u32[]{:S(2)}) async-start(f32[32,2,12,96]{3,1,2,0:T(2,128)} %broadcast_in_dim.8), calls=%async_computation | async-start | bytes 786432 | tf_op jit(solution)/shard_map/all_to_all | solution.py:24
  57.9 55.7 %all-gather.3.cloned.1.call-start = ((), (), s32[]{:S(2)}) async-start(), calls=%async_computation.4 | async-start | bytes 2949120 | tf_op jit(solution)/shard_map/all_gather | solution.py:13
  58.8 2.6 copy-start.2
  58.9 2.1 copy-start.5
  58.9 2.3 copy-start.8
  109.2 12.2 %all-to-all-start.1 = ((f32[2,384,96]{2,0,1:T(2,128)}), f32[2,384,96]{2,0,1:T(2,128)S(1)}, u32[]{:S(2)}, u32[]{:S(2)}) async-start(f32[2,384,96]{2,0,1:T(2,128)} %bitcast.19), calls=%async_computation.1 | async-start | bytes 786432 | tf_op jit(solution)/shard_map/all_to_all | solution.py:94
  113.5 156.3 %all-gather.5.cloned.1.call-start = ((), (), s32[]{:S(2)}) async-start(), calls=%async_computation.5 | async-start | bytes 4866048 | tf_op jit(solution)/shard_map/all_gather | solution.py:145
  119.9 2.0 copy-start.9
  121.4 1.0 copy-start.13
  122.4 14.8 %copy-start.12 = (bf16[64,128]{1,0:T(8,128)(2,1)S(1)}, bf16[64,128]{1,0:T(8,128)(2,1)}, u32[]{:S(2)}) copy-start(bf16[64,128]{1,0:T(8,128)(2,1)} %param.20) | copy-start | bytes 49156
  146.0 0.7 copy-start.3
  299.2 24.6 %copy-start.4 = (bf16[12,48,128]{2,1,0:T(8,128)(2,1)S(1)}, bf16[12,48,128]{2,1,0:T(8,128)(2,1)}, u32[]{:S(2)}) copy-start(bf16[12,48,128]{2,1,0:T(8,128)(2,1)} %copy-done.3) | copy-start | bytes 442372
  299.2 24.6 %copy-start.11 = (bf16[128,128]{1,0:T(8,128)(2,1)S(1)}, bf16[128,128]{1,0:T(8,128)(2,1)}, u32[]{:S(2)}) copy-start(bf16[128,128]{1,0:T(8,128)(2,1)} %param.22) | copy-start | bytes 98308
  299.2 41.0 %all-to-all-start.3 = ((bf16[8,12,48,128]{3,2,1,0:T(8,128)(2,1)}), bf16[8,12,48,128]{3,2,1,0:T(8,128)(2,1)S(1)}, u32[]{:S(2)}, u32[]{:S(2)}) async-start(bf16[8,12,48,128]{3,2,1,0:T(8,128)(2,1)} %copy.84), calls=%async_computation.3 | async-start | bytes 2359296 | tf_op jit(solution)/shard_map/all_to_all | solution.py:40
  323.9 17.3 %copy-start.7 = (bf16[128,128]{1,0:T(8,128)(2,1)S(1)}, bf16[128,128]{1,0:T(8,128)(2,1)}, u32[]{:S(2)}) copy-start(bf16[128,128]{1,0:T(8,128)(2,1)} %param.23) | copy-start | bytes 98308
  340.8 1.2 copy-start.10
Sparse Core Ops, SparseCore 0:
  60.8 50.1 all-gather.2
  148.0 121.8 all-gather.4
where the time goes:
time: 351 us; the launch traced here: 350 us
  waiting for transfers between devices  185 us (53%)
  starting transfers between devices  75.3 us (21%)
  local copies, waits for them, and re-layouts  32.7 us (9%)
  matrix products  28.6 us (8%)
  between operations  14.5 us (4%)
  other arithmetic  6.71 us (2%)
  blocking collectives  6.71 us (2%)
    all_gather x1, waiting for transfers between devices, local(): lax.all_gather(right, 'row', axis=0, tiled=True)  122 us
    all_to_all x1, waiting for transfers between devices, copy_for_each(): lax.all_to_all(jnp.broadcast_to(shard[None], (devices, *shard.shape)), ax...  47.7 us
    all_to_all x1, starting transfers between devices, copy_for_each(): lax.all_to_all(jnp.broadcast_to(shard[None], (devices, *shard.shape)), ax...  46.3 us
    all_to_all x1, starting transfers between devices, sum_at_owner(): lax.all_to_all(cut_along(shard, dim, devices), axis, 0, 0, tiled=True)  24.6 us
    all_gather x1, local copies, waits for them, and re-layouts, local(): lax.all_gather(right, 'row', axis=0, tiled=True)  17.9 us
    all_to_all x1, waiting for transfers between devices, sum_at_owner(): lax.all_to_all(cut_along(shard, dim, devices), axis, 0, 0, tiled=True)  16.1 us
    dot_general x6, matrix products, attend(): jnp.einsum('ahjk,akhd->ajhd', weights, block_values, preferred_element_ty...  10.1 us
    dot_general x1, matrix products, local(): jnp.einsum('ikc,jkc->ijc', left, lax.all_gather(right, 'row', axis=0, til...  9.04 us
  transfers between devices with their start and end apart: 5, of which 3 were waited for; matrix products, arithmetic and copies ran while one was open for 3% of the time, Pallas kernels for 0%

commit v1 on v0

--- a/solution.py
+++ b/solution.py
@@ -1,7 +1,14 @@
+import functools
+
 import jax
 import jax.numpy as jnp
 from jax import lax
+from jax.experimental import pallas as pl
+from jax.experimental.pallas import tpu as pltpu
 from jax.sharding import PartitionSpec as P
+
+MESH = pl.DeviceIdType.MESH
+CHUNKS = 4
 
 
 def sent_together(arrays, axis, dim, along):
@@ -46,6 +53,231 @@
     centred = value - mean
     variance = jnp.mean(centred * centred, axis=-1, keepdims=True)
     return centred * lax.rsqrt(variance + 1e-05)
+
+
+def tail_kernel(
+    n_row,
+    n_col,
+    n_sub,
+    length_ref,
+    first_ref,
+    mult_in_ref,
+    mult_gate_ref,
+    mult_out_ref,
+    trans_up_ref,
+    trans_down_ref,
+    out_ref,
+    gathered,
+    left,
+    stage_f32,
+    stage,
+    parts,
+    tri,
+    gate,
+    ring_send,
+    ring_recv,
+    part_send,
+    part_recv,
+):
+    rows, half, width = first_ref.shape
+    piece = rows // CHUNKS
+    z = lax.axis_index("row")
+    x = lax.axis_index("col")
+    core = lax.axis_index("sub")
+    owners = n_col * n_sub
+    me = x * n_sub + core
+    per_owner = n_row // owners
+    far = n_row // 2
+    up = lax.rem(z + 1, n_row)
+    down = lax.rem(z + n_row - 1, n_row)
+
+    barrier = pltpu.get_barrier_semaphore()
+    for other in (up, down):
+        pl.semaphore_signal(barrier, inc=1, device_id={"row": other}, device_id_type=MESH)
+    for step in range(1, owners):
+        other = lax.rem(me + step, owners)
+        pl.semaphore_signal(
+            barrier,
+            inc=1,
+            device_id={"col": lax.div(other, n_sub), "sub": lax.rem(other, n_sub)},
+            device_id_type=MESH,
+        )
+
+    first = first_ref[...].reshape(rows * half, width)
+    mixed = norm(first).astype(jnp.bfloat16)
+    quad = jnp.dot(mixed, mult_in_ref[...], preferred_element_type=jnp.float32)
+    shape = (rows, half, width)
+    here_row = z * rows + lax.broadcasted_iota(jnp.int32, shape, 0)
+    here_col = (x * n_sub + core) * half + lax.broadcasted_iota(jnp.int32, shape, 1)
+    length = length_ref[0]
+    valid = ((here_row < length) & (here_col < length)).astype(jnp.float32)
+    a, b, c, d = [quad[:, k * width : (k + 1) * width].reshape(shape) for k in range(4)]
+    left[...] = (valid * jax.nn.sigmoid(b) * a).astype(jnp.bfloat16).astype(jnp.float32)
+    gathered[z] = (valid * jax.nn.sigmoid(d) * c).astype(jnp.bfloat16)
+    gate[...] = jax.nn.sigmoid(
+        jnp.dot(mixed, mult_gate_ref[...], preferred_element_type=jnp.float32)
+    )
+    pl.semaphore_wait(barrier, 2 + owners - 1)
+
+    def source(way, step):
+        return lax.rem(z + (n_row - step if way == 0 else step), n_row)
+
+    def ring_copy(way, step, chunk, arrives):
+        block = gathered.at[source(way, step), pl.ds(chunk * piece, piece)]
+        return pltpu.make_async_remote_copy(
+            src_ref=block,
+            dst_ref=block,
+            send_sem=ring_send.at[way, lax.rem(step, 2), chunk],
+            recv_sem=ring_recv.at[way, step - 1 if arrives else step, chunk],
+            device_id={"row": up if way == 0 else down},
+            device_id_type=MESH,
+        )
+
+    def hop(way, step, chunk):
+        return ring_copy(way, step, chunk, False)
+
+    def arrival(way, step, chunk):
+        return ring_copy(way, step, chunk, True)
+
+    def multiply(owner, chunk, lane):
+        for jj in range(piece):
+            j = chunk * piece + jj
+            right = gathered[owner, j].astype(jnp.float32)
+            for i in range(rows):
+                stage_f32[lane, pl.ds(i * rows + j, 1)] = jnp.sum(
+                    left[i] * right, axis=0, keepdims=True
+                )
+
+    def part_copy(block):
+        dest = lax.div(block, per_owner)
+        slot = lax.rem(block, per_owner)
+        return pltpu.make_async_remote_copy(
+            src_ref=stage.at[block],
+            dst_ref=parts.at[me, slot],
+            send_sem=part_send.at[block],
+            recv_sem=part_recv.at[me, slot],
+            device_id={"col": lax.div(dest, n_sub), "sub": lax.rem(dest, n_sub)},
+            device_id_type=MESH,
+        )
+
+    def give(block, lane):
+        slot = lax.rem(block, per_owner)
+        mine = lax.div(block, per_owner) == me
+        stage[block] = stage_f32[lane].astype(jnp.bfloat16)
+
+        @pl.when(mine)
+        def _():
+            pltpu.make_async_copy(
+                stage.at[block], parts.at[me, slot], part_recv.at[me, slot]
+            ).start()
+
+        @pl.when(jnp.logical_not(mine))
+        def _():
+            part_copy(block).start()
+
+    for chunk in range(CHUNKS):
+        for way in range(2):
+            hop(way, 0, chunk).start()
+
+    def own(chunk, carry):
+        multiply(z, chunk, 0)
+        return carry
+
+    lax.fori_loop(0, CHUNKS, own, 0)
+    give(z, 0)
+
+    def visit(n, carry):
+        step = lax.div(n, CHUNKS) + 1
+        chunk = lax.rem(n, CHUNKS)
+        for way in range(2):
+            arrival(way, step, chunk).wait_recv()
+            last = chunk < CHUNKS // 2 if way == 0 else chunk >= CHUNKS // 2
+
+            @pl.when(step >= 2)
+            def _():
+                hop(way, step, chunk).wait_send()
+
+            @pl.when(jnp.logical_or(step < far - 1, last))
+            def _():
+                hop(way, step, chunk).start()
+
+        for way in range(2):
+            multiply(source(way, step), chunk, way)
+
+        @pl.when(chunk == CHUNKS - 1)
+        def _():
+            for way in range(2):
+                give(source(way, step), way)
+
+        return carry
+
+    lax.fori_loop(0, (far - 1) * CHUNKS, visit, 0)
+
+    for chunk in range(CHUNKS):
+        arrival(0 if chunk < CHUNKS // 2 else 1, far, chunk).wait_recv()
+        multiply(source(0, far), chunk, 0)
+    give(source(0, far), 0)
+
+    for way in range(2):
+        for chunk in range(CHUNKS):
+            hop(way, far - 2, chunk).wait_send()
+            if (chunk < CHUNKS // 2) == (way == 0):
+                hop(way, far - 1, chunk).wait_send()
+
+    for block in range(n_row):
+
+        @pl.when(block // per_owner != me)
+        def _():
+            part_copy(block).wait_send()
+
+    for slot in range(per_owner):
+        total = None
+        for giver in range(owners):
+            pltpu.make_async_copy(
+                stage.at[0], parts.at[giver, slot], part_recv.at[giver, slot]
+            ).wait()
+            part = parts[giver, slot].astype(jnp.float32)
+            total = part if total is None else total + part
+        for i in range(rows):
+            tri[i, slot * rows : (slot + 1) * rows] = total[i * rows : (i + 1) * rows]
+
+    tri_normed = norm(tri[...].reshape(rows * half, width)).astype(jnp.bfloat16)
+    second = first_ref[...].reshape(rows * half, width) + gate[...] * jnp.dot(
+        tri_normed, mult_out_ref[...], preferred_element_type=jnp.float32
+    )
+    last_normed = norm(second).astype(jnp.bfloat16)
+    hidden = jax.nn.relu(
+        jnp.dot(last_normed, trans_up_ref[...], preferred_element_type=jnp.float32)
+    ).astype(jnp.bfloat16)
+    result = second + jnp.dot(hidden, trans_down_ref[...], preferred_element_type=jnp.float32)
+    out_ref[...] = result.astype(jnp.bfloat16).reshape(rows, half, width)
+
+
+def tail(first, length, mult_in, mult_gate, mult_out, trans_up, trans_down):
+    rows, half, width = first.shape
+    n_row, n_col, n_sub = (lax.axis_size(a) for a in ("row", "col", "sub"))
+    owners = n_col * n_sub
+    vmem = pl.BlockSpec(memory_space=pltpu.VMEM)
+    return pl.pallas_call(
+        functools.partial(tail_kernel, n_row, n_col, n_sub),
+        out_shape=jax.ShapeDtypeStruct(first.shape, jnp.bfloat16),
+        in_specs=[pl.BlockSpec(memory_space=pltpu.SMEM)] + [vmem] * 6,
+        out_specs=vmem,
+        scratch_shapes=[
+            pltpu.VMEM((n_row, rows, half, width), jnp.bfloat16),
+            pltpu.VMEM((rows, half, width), jnp.float32),
+            pltpu.VMEM((2, rows * rows, width), jnp.float32),
+            pltpu.VMEM((n_row, rows * rows, width), jnp.bfloat16),
+            pltpu.VMEM((owners, n_row // owners, rows * rows, width), jnp.bfloat16),
+            pltpu.VMEM((rows, half, width), jnp.float32),
+            pltpu.VMEM((rows * half, width), jnp.float32),
+            pltpu.SemaphoreType.DMA((2, 2, CHUNKS)),
+            pltpu.SemaphoreType.DMA((2, n_row // 2, CHUNKS)),
+            pltpu.SemaphoreType.DMA((n_row,)),
+            pltpu.SemaphoreType.DMA((owners, n_row // owners)),
+        ],
+        compiler_params=pltpu.CompilerParams(collective_id=0, has_side_effects=True),
+    )(length, first, mult_in, mult_gate, mult_out, trans_up, trans_down)
 
 
 def local(
@@ -65,7 +297,6 @@
     rows, cols, width = pair.shape
     row_count = lax.axis_size("row")
     sub_count = lax.axis_size("sub")
-    row_index = lax.axis_index("row")
     col_index = lax.axis_index("col")
     sub_index = lax.axis_index("sub")
     total = rows * row_count
@@ -73,7 +304,6 @@
     heads_here = att_bias.shape[1]
     spread = att_out.shape[0]
     head_dim = spread // heads_here
-    mult_width = mult_out.shape[0]
     valid = (jnp.arange(total) < length[0]).astype(jnp.float32)
     normed = norm(pair.astype(jnp.float32)).astype(jnp.bfloat16)
     flat = normed.reshape(rows * cols, width)
@@ -128,36 +358,7 @@
     update_half = sum_at_owner(update.astype(jnp.bfloat16), "sub", 1)
     pair_half = lax.dynamic_slice_in_dim(pair, sub_index * half, half, 1).astype(jnp.float32)
     first = pair_half + update_half
-    mixed = norm(first).astype(jnp.bfloat16)
-    mixed_flat = mixed.reshape(rows * half, width)
-    quad = jnp.dot(mixed_flat, mult_in, preferred_element_type=jnp.float32).reshape(
-        rows, half, 4, mult_width
-    )
-    row_valid = lax.dynamic_slice_in_dim(valid, row_index * rows, rows, 0)
-    col_valid = lax.dynamic_slice_in_dim(valid, col_index * cols + sub_index * half, half, 0)
-    outer = row_valid[:, None, None] * col_valid[None, :, None]
-    left = (outer * jax.nn.sigmoid(quad[:, :, 1]) * quad[:, :, 0]).astype(jnp.bfloat16)
-    right = (outer * jax.nn.sigmoid(quad[:, :, 3]) * quad[:, :, 2]).astype(jnp.bfloat16)
-    gate_out = jax.nn.sigmoid(jnp.dot(mixed_flat, mult_gate, preferred_element_type=jnp.float32))
-    partial_value = jnp.einsum(
-        "ikc,jkc->ijc",
-        left,
-        lax.all_gather(right, "row", axis=0, tiled=True),
-        preferred_element_type=jnp.float32,
-    )
-    tri = sum_at_owner(partial_value.astype(jnp.bfloat16), ("col", "sub"), 1)
-    tri_normed = norm(tri).astype(jnp.bfloat16).reshape(rows * half, mult_width)
-    second = first + (
-        gate_out * jnp.dot(tri_normed, mult_out, preferred_element_type=jnp.float32)
-    ).reshape(rows, half, width)
-    last_normed = norm(second).astype(jnp.bfloat16).reshape(rows * half, width)
-    hidden = jax.nn.relu(jnp.dot(last_normed, trans_up, preferred_element_type=jnp.float32)).astype(
-        jnp.bfloat16
-    )
-    result = second + jnp.dot(hidden, trans_down, preferred_element_type=jnp.float32).reshape(
-        rows, half, width
-    )
-    return result.astype(jnp.bfloat16)
+    return tail(first, length, mult_in, mult_gate, mult_out, trans_up, trans_down)
 
 
 def solution(mesh):

time: 351 us -> 238 us (0.68)
  the two profiles are of different devices: /device:TPU:33 before, /device:TPU:36 now
where the time goes in v1:
time: 238 us; the launch traced here: 237 us
  Pallas kernels  75.4 us (32%)
  starting transfers between devices  50.7 us (21%)
  waiting for transfers between devices  48.7 us (20%)
  matrix products  27.4 us (12%)
  between operations  14.3 us (6%)
  local copies, waits for them, and re-layouts  11.2 us (5%)
  other arithmetic  5.08 us (2%)
  blocking collectives  3.97 us (2%)
    pallas_call x1, Pallas kernels, tail(): pl.pallas_call(functools.partial(tail_kernel, n_row, n_col, n_sub), out_s...  75.4 us
    all_to_all x1, waiting for transfers between devices, copy_for_each(): lax.all_to_all(jnp.broadcast_to(shard[None], (devices, *shard.shape)), ax...  48.7 us
    all_to_all x1, starting transfers between devices, copy_for_each(): lax.all_to_all(jnp.broadcast_to(shard[None], (devices, *shard.shape)), ax...  45.8 us
    dot_general x6, matrix products, attend(): jnp.einsum('ahjk,akhd->ajhd', weights, block_values, preferred_element_ty...  10.1 us
    sub x6, matrix products, attend(): weights = jax.nn.softmax(scores, axis=-1).astype(jnp.bfloat16)  7.36 us
    dot_general x6, matrix products, attend(): jnp.einsum('ajhd,akhd->ahjk', block_query, block_keys, preferred_element_...  6.31 us
    unnamed x19, local copies, waits for them, and re-layouts  4.92 us
    all_to_all x1, starting transfers between devices, local(): lax.all_to_all(column_bias, 'col', split_axis=1, concat_axis=2, tiled=True)  4.81 us
  transfers between devices with their start and end apart: 3, of which 1 were waited for; matrix products, arithmetic and copies ran while one was open for 4% of the time, Pallas kernels for 0%

profile of v1, /device:TPU:36, one launch (start us, length us, event | category | flops | bytes accessed | tf_op | source)
XLA Modules:
  0.0 236.8 jit_solution(8170852924888150554)
XLA Ops:
  6.6 1.2 convert_reduce_fusion
  7.8 1.4 fusion.22
  9.2 1.4 convolution_bitcast_fusion.1
  11.5 45.8 %all-to-all-start = ((f32[32,2,12,96]{3,1,2,0:T(2,128)}), f32[32,2,12,96]{3,1,2,0:T(2,128)}, u32[]{:S(2)}, u32[]{:S(2)}) async-start(f32[32,2,12,96]{3,1,2,0:T(2,128)} %broadcast_in_dim.8), calls=%async_computation | async-start | bytes 786432 | tf_op jit(solution)/shard_map/all_to_all | solution.py:31
  58.4 1.2 copy.28
  61.9 48.7 %all-to-all-done = f32[32,2,12,96]{3,1,2,0:T(2,128)} async-done(((f32[32,2,12,96]{3,1,2,0:T(2,128)}), f32[32,2,12,96]{3,1,2,0:T(2,128)}, u32[]{:S(2)}, u32[]{:S(2)}) %all-to-all-start) | async-done | bytes 294944 | tf_op jit(solution)/shard_map/all_to_all | solution.py:31
  110.6 4.8 %all-to-all-start.1 = ((f32[2,384,96]{2,0,1:T(2,128)}), f32[2,384,96]{2,0,1:T(2,128)}, u32[]{:S(2)}, u32[]{:S(2)}) async-start(f32[2,384,96]{2,0,1:T(2,128)} %bitcast.19), calls=%async_computation.1 | async-start | bytes 786432 | tf_op jit(solution)/shard_map/all_to_all | solution.py:324
  115.4 2.6 %fusion.45 = (bf16[12,384,64]{2,0,1:T(8,128)(2,1)S(1)}, bf16[12,384,64]{2,0,1:T(8,128)(2,1)S(1)}) fusion(bf16[24,384,64]{2,0,1:T(8,128)(2,1)} %all-gather.2.cloned.1.call-done), kind=kLoop, calls=%fused_computation.55 | loop fusion | bytes 2359296 | tf_op jit(solution)/shard_map/split | solution.py:20
  118.0 1.8 copy.38
  119.8 1.5 copy.39
  121.3 1.3 copy.42
  123.0 23.8 %while.10 = (s32[]{:T(128)}, f32[6,2,96,2,32]{2,4,3,1,0:T(8,128)S(1)}, bf16[6,2,384,2,32]{2,4,3,1,0:T(8,128)(2,1)}, bf16[6,2,96,2,32]{2,4,3,1,0:T(8,128)(2,1)}, ...) while((s32[]{:T(128)}, f32[6,2,96,2,32]{2,4,3,1,0:T(8,128)S(1)}, ...), condition=%wide.region_5.6_spmd, body=%wide.region_2.5_spmd.sunk | while | flops 29344896 | bytes 2792013 | solution.py:346
  124.0 1.2 fusion.62
  125.3 1.7 fusion.63
  127.0 1.1 convolution_add_fusion.2
  128.0 1.2 fusion.62
  129.2 1.7 fusion.63
  132.0 1.2 fusion.62
  133.2 1.7 fusion.63
  134.9 1.1 convolution_add_fusion.2
  136.0 1.2 fusion.62
  137.2 1.7 fusion.63
  138.9 1.1 convolution_add_fusion.2
  139.9 1.2 fusion.62
  141.2 1.7 fusion.63
  142.9 1.1 convolution_add_fusion.2
  143.9 1.2 fusion.62
  145.1 1.7 fusion.63
  146.8 1.3 convolution_convert_fusion
  148.2 4.0 %all_to_all.28 = bf16[2,12,48,128]{3,2,1,0:T(8,128)(2,1)S(1)} all-to-all(bf16[2,12,48,128]{3,2,1,0:T(8,128)(2,1)S(1)} %bitcast.97), channel_id=1, replica_groups=mesh['grp'=2,'row'=32,'col'=4,'sub'=2] {'sub'}, dimensions={0} | all-to-all | bytes 589824 | tf_op jit(solution)/shard_map/all_to_all | solution.py:47
  152.9 75.4 %shard_map.118 = bf16[12,48,128]{2,1,0:T(8,128)(2,1)} custom-call(s32[1]{0:T(128)} %copy.52.length_ref, f32[12,48,128]{2,1,0:T(8,128)} %convert_add_fusion.first_ref, bf16[128,512]{1,0:T(8,128)(2,1)} %mult_in_ref.1, bf16[128,128]{1,0:T(8,128)(2,1)} %mult_gate_ref.1, bf16[128,128]{1,0:T(8,128)(2,1)} %mult_out_ref.1, bf16[128,512]{1,0:T(8,128)(2,1)} %trans_up_ref.1, ...), custom_call_target="tpu_custom_call" | custom-call | tf_op jit(solution)/shard_map/pallas_call | solution.py:261
  228.3 1.6 copy.54
  (38 shorter events, 6.8 us)
Async XLA Ops:
  6.5 50.9 %copy-start = (bf16[128,4,64]{0,2,1:T(8,128)(2,1)S(1)}, bf16[128,4,64]{0,2,1:T(8,128)(2,1)}, u32[]{:S(2)}) copy-start(bf16[128,4,64]{0,2,1:T(8,128)(2,1)} %param.17) | copy-start | bytes 196612
  6.6 50.9 %copy-start.1 = (bf16[12,96,128]{2,1,0:T(8,128)(2,1)S(1)}, bf16[12,96,128]{2,1,0:T(8,128)(2,1)}, u32[]{:S(2)}) copy-start(bf16[12,96,128]{2,1,0:T(8,128)(2,1)} %param.14) | copy-start | bytes 884740
  11.5 99.0 %all-to-all-start = ((f32[32,2,12,96]{3,1,2,0:T(2,128)}), f32[32,2,12,96]{3,1,2,0:T(2,128)}, u32[]{:S(2)}, u32[]{:S(2)}) async-start(f32[32,2,12,96]{3,1,2,0:T(2,128)} %broadcast_in_dim.8), calls=%async_computation | async-start | bytes 786432 | tf_op jit(solution)/shard_map/all_to_all | solution.py:31
  57.3 58.1 %all-gather.2.cloned.1.call-start = ((), (), s32[]{:S(2)}) async-start(), calls=%async_computation.3 | async-start | bytes 2949120 | tf_op jit(solution)/shard_map/all_gather | solution.py:20
  58.3 2.9 %copy-start.2 = (f32[12,96,4,64]{1,3,2,0:T(8,128)}, f32[12,96,4,64]{1,3,2,0:T(8,128)S(1)}, u32[]{:S(2)}) copy-start(f32[12,96,4,64]{1,3,2,0:T(8,128)S(1)} %get-tuple-element.61) | copy-start | bytes 3538948
  58.3 2.0 copy-start.4
  110.6 10.7 %all-to-all-start.1 = ((f32[2,384,96]{2,0,1:T(2,128)}), f32[2,384,96]{2,0,1:T(2,128)}, u32[]{:S(2)}, u32[]{:S(2)}) async-start(f32[2,384,96]{2,0,1:T(2,128)} %bitcast.19), calls=%async_computation.1 | async-start | bytes 786432 | tf_op jit(solution)/shard_map/all_to_all | solution.py:324
  119.8 3.1 %copy-start.3 = (f32[96,384]{1,0:T(8,128)S(1)}, f32[96,384]{1,0:T(8,128)}, u32[]{:S(2)}) copy-start(f32[96,384]{1,0:T(8,128)} %compare_convert_fusion) | copy-start | bytes 442372
  119.8 3.1 %copy-start.5 = (f32[2]{0:T(128)S(1)}, f32[2]{0:T(128)}, u32[]{:S(2)}) copy-start(f32[2]{0:T(128)} %param.19) | copy-start | bytes 28
  121.3 1.7 copy-start.7
  123.0 23.9 %copy-start.6 = (bf16[64,128]{1,0:T(8,128)(2,1)S(1)}, bf16[64,128]{1,0:T(8,128)(2,1)}, u32[]{:S(2)}) copy-start(bf16[64,128]{1,0:T(8,128)(2,1)} %param.20) | copy-start | bytes 49156
Sparse Core Ops, SparseCore 0:
  60.3 48.6 all-gather.1

commit v2 on v1

v2 whole, which is shorter than its diff:
```python
import functools

import jax
import jax.numpy as jnp
from jax import lax
from jax.experimental import pallas as pl
from jax.experimental.pallas import tpu as pltpu
from jax.sharding import PartitionSpec as P

MESH = pl.DeviceIdType.MESH
CHUNKS = 4
STRIDE = 4
LOCAL = (-1, 1, 2)


def norm(value):
    mean = jnp.mean(value, axis=-1, keepdims=True)
    centred = value - mean
    variance = jnp.mean(centred * centred, axis=-1, keepdims=True)
    return centred * lax.rsqrt(variance + 1e-05)


def pair_kernel(
    n_row,
    n_col,
    n_sub,
    length_ref,
    chain_ref,
    chain_bias_ref,
    pair_ref,
    chain_cols_ref,
    bias_w_ref,
    att_w_ref,
    att_out_ref,
    mult_in_ref,
    mult_gate_ref,
    mult_out_ref,
    trans_up_ref,
    trans_down_ref,
    out_ref,
    normed,
    kept,
    queries,
    att_gate,
    scores,
    bias,
    pieces,
    bias_in,
    other_w,
    both_out,
    attended,
    first_ref,
    gathered,
    left,
    stage_f32,
    stage,
    parts,
    tri,
    gate,
    x_send,
    x_recv,
    weight_send,
    weight_recv,
    chain_send,
    chain_recv,
    bias_send,
    bias_recv,
    ring_send,
    ring_recv,
    part_send,
    part_recv,
):
    rows, cols, width = pair_ref.shape
    half = cols // n_sub
    total = rows * n_row
    piece = rows // CHUNKS
    block_rows = rows // 2
    heads_here = pieces.shape[1] // rows
    heads = heads_here * n_sub
    head_dim = width // heads
    z = lax.axis_index("row")
    x = lax.axis_index("col")
    core = lax.axis_index("sub")
    owners = n_col * n_sub
    me = x * n_sub + core
    per_owner = n_row // owners
    far = n_row // 2
    up = lax.rem(z + 1, n_row)
    down = lax.rem(z + n_row - 1, n_row)
    length = length_ref[0]

    def row_at(offset):
        return lax.rem(z + (offset + n_row), n_row)

    barrier = pltpu.get_barrier_semaphore()
    near = (1, -1, 2, -2, STRIDE, -STRIDE)
    for offset in near:
        pl.semaphore_signal(
            barrier, inc=1, device_id={"row": row_at(offset)}, device_id_type=MESH
        )
    for step in range(1, owners):
        other = lax.rem(me + step, owners)
        pl.semaphore_signal(
            barrier,
            inc=1,
            device_id={"col": lax.div(other, n_sub), "sub": lax.rem(other, n_sub)},
            device_id_type=MESH,
        )

    normed[x] = norm(pair_ref[...].astype(jnp.float32)).astype(jnp.bfloat16)
    both_out[core] = att_out_ref[...]

    lane = lax.broadcasted_iota(jnp.int32, (8, width), 1)
    line = lax.broadcasted_iota(jnp.int32, (8, width), 0)
    chain_bias = jnp.zeros((8, width), jnp.float32)
    for h in range(heads_here):
        chain_bias = jnp.where(line == h, chain_bias_ref[h], chain_bias)
    key_valid = ((x * cols + lane) < length).astype(jnp.float32)
    padding = jnp.zeros((width - cols, width), jnp.bfloat16)
    for i in range(rows):
        keys_i = jnp.concatenate([normed[x, i], padding], axis=0)
        term = lax.dot_general(
            bias_w_ref[...], keys_i, (((1,), (1,)), ((), ())), preferred_element_type=jnp.float32
        )
        same = (chain_cols_ref[...] == chain_ref[z * rows + i]).astype(jnp.float32)
        term = term + chain_bias * same + (key_valid - 1.0) * 1000000000.0
        term = pltpu.roll(term, lax.rem(x * cols, width), 1)
        for h in range(heads_here):
            pieces[z, h * rows + i : h * rows + i + 1] = term[h : h + 1]

    pl.semaphore_wait(barrier, len(near) + owners - 1)

    def weight_copy(k):
        source, target = [(att_w_ref, other_w), (both_out.at[core], both_out.at[core])][k]
        return pltpu.make_async_remote_copy(
            src_ref=source,
            dst_ref=target,
            send_sem=weight_send.at[k],
            recv_sem=weight_recv.at[k],
            device_id={"sub": 1 - core},
            device_id_type=MESH,
        )

    def x_copy(way, step, chunk, arrives):
        distance = step + 1 if arrives else step
        source = lax.rem(x + (n_col - distance if way == 0 else distance), n_col)
        block = normed.at[source, pl.ds(chunk * block_rows, block_rows)]
        return pltpu.make_async_remote_copy(
            src_ref=block,
            dst_ref=block,
            send_sem=x_send.at[way, step, chunk],
            recv_sem=x_recv.at[way, step, chunk],
            device_id={"col": lax.rem(x + (1 if way == 0 else n_col - 1), n_col)},
            device_id_type=MESH,
        )

    def bias_hop(stop, k, block, offset):
        return pltpu.make_async_remote_copy(
            src_ref=pieces.at[block],
            dst_ref=pieces.at[block],
            send_sem=chain_send.at[stop, k],
            recv_sem=chain_recv.at[block],
            device_id={"row": row_at(offset)},
            device_id_type=MESH,
        )

    def owner_copy(block, source, target, send_sem, recv_sem):
        dest = lax.div(block, per_owner)
        return pltpu.make_async_remote_copy(
            src_ref=source.at[block],
            dst_ref=target.at[me, lax.rem(block, per_owner)],
            send_sem=send_sem.at[block],
            recv_sem=recv_sem.at[me, lax.rem(block, per_owner)],
            device_id={"col": lax.div(dest, n_sub), "sub": lax.rem(dest, n_sub)},
            device_id_type=MESH,
        )

    def to_owner(block, source, target, send_sem, recv_sem):
        slot = lax.rem(block, per_owner)
        mine = lax.div(block, per_owner) == me

        @pl.when(mine)
        def _():
            pltpu.make_async_copy(
                source.at[block], target.at[me, slot], recv_sem.at[me, slot]
            ).start()

        @pl.when(jnp.logical_not(mine))
        def _():
            owner_copy(block, source, target, send_sem, recv_sem).start()

    bias_way = (pieces, bias_in, bias_send, bias_recv)
    part_way = (stage, parts, part_send, part_recv)
    ups = n_row // (2 * STRIDE)

    def hops_of(stop):
        if stop == 0:
            ahead = [(0, STRIDE), (len(LOCAL) + 1, -STRIDE)]
        elif stop < ups:
            ahead = [(0, STRIDE)]
        elif stop == ups or stop == 2 * ups - 1:
            ahead = []
        else:
            ahead = [(0, -STRIDE)]
        return ahead + [(1 + n, offset) for n, offset in enumerate(LOCAL)]

    def block_of(stop):
        return row_at(-STRIDE * stop if stop <= ups else STRIDE * (stop - ups))

    def pass_on(stop):
        block = block_of(stop)
        if stop > 0:
            bias_hop(stop, 0, block, 0).wait_recv()
        for k, offset in hops_of(stop):
            bias_hop(stop, k, block, offset).start()
        to_owner(block, *bias_way)

    def take_local(stop):
        for offset in LOCAL:
            block = lax.rem(block_of(stop) + (n_row - offset), n_row)
            bias_hop(stop, 0, block, 0).wait_recv()
            to_owner(block, *bias_way)

    def project(source, chunk):
        tile = normed[source, pl.ds(chunk * block_rows, block_rows)]
        made = jnp.dot(
            tile.reshape(block_rows * cols, width),
            w_all[:, width : 3 * width],
            preferred_element_type=jnp.float32,
        ).astype(jnp.bfloat16)
        kept[
            pl.ds(chunk * block_rows, block_rows), pl.ds(pl.multiple_of(source * cols, 32), cols)
        ] = made.reshape(block_rows, cols, 2 * width)

    def score(i, carry):
        scores[i] = lax.dot_general(
            queries[i],
            kept[i, :, :width],
            (((1,), (1,)), ((), ())),
            preferred_element_type=jnp.float32,
        )
        return carry

    pass_on(0)
    for k in range(2):
        weight_copy(k).start()
    for chunk in range(2):
        for way in range(2):
            x_copy(way, 0, chunk if way == 0 else 1 - chunk, False).start()

    for k in range(2):
        weight_copy(k).wait_recv()
    w_all = att_w_ref[...] + other_w[...]
    tile = normed[x, :, pl.ds(pl.multiple_of(core * half, 16), half)].reshape(rows * half, width)
    query = (
        jnp.dot(tile, w_all[:, :width], preferred_element_type=jnp.float32) * head_dim ** (-0.5)
    ).astype(jnp.bfloat16)
    head_of = lax.broadcasted_iota(jnp.int32, (rows * half, width), 1) // head_dim
    for h in range(heads):
        queries[:, h * half : (h + 1) * half] = jnp.where(
            head_of == h, query, jnp.zeros_like(query)
        ).reshape(rows, half, width)
    att_gate[...] = jax.nn.sigmoid(
        jnp.dot(tile, w_all[:, 3 * width :], preferred_element_type=jnp.float32)
    ).reshape(rows, half, width)
    for chunk in range(2):
        project(x, chunk)

    x_up = lax.rem(x + n_col - 1, n_col)
    x_down = lax.rem(x + 1, n_col)
    x_far = lax.rem(x + 2, n_col)

    def stage_of(step):
        if step <= ups:
            pass_on(step)
        if step < ups:
            pass_on(ups + step)
        take_local(step - 1)
        if 1 <= step - 1 < ups:
            take_local(ups + step - 1)

    stage_of(1)
    x_copy(0, 0, 0, True).wait_recv()
    x_copy(0, 1, 0, False).start()
    x_copy(1, 0, 1, True).wait_recv()
    x_copy(1, 1, 1, False).start()
    project(x_up, 0)
    project(x_down, 1)
    stage_of(2)
    x_copy(0, 0, 1, True).wait_recv()
    project(x_up, 1)
    x_copy(1, 0, 0, True).wait_recv()
    project(x_down, 0)
    stage_of(3)
    x_copy(0, 1, 0, True).wait_recv()
    project(x_far, 0)
    lax.fori_loop(0, block_rows, score, 0)
    stage_of(4)
    x_copy(1, 1, 1, True).wait_recv()
    project(x_far, 1)
    lax.fori_loop(block_rows, rows, score, 0)
    take_local(ups)

    for slot in range(per_owner):
        for giver in range(owners):
            pltpu.make_async_copy(
                pieces.at[0], bias_in.at[giver, slot], bias_recv.at[giver, slot]
            ).wait()
    lane = lax.broadcasted_iota(jnp.int32, (rows, width), 1)
    for slot in range(per_owner):
        for h in range(heads):
            giver, own_head = h // heads_here, h % heads_here
            held = [
                bias_in[k * n_sub + giver, slot, own_head * rows : (own_head + 1) * rows]
                for k in range(n_col)
            ]
            at = h * half + slot * rows
            for k in range(total // width):
                line = None
                for source in range(n_col):
                    begin = source * cols - k * width
                    if begin + cols <= 0 or begin >= width:
                        continue
                    line = held[source] if line is None else jnp.where(lane >= begin, held[source], line)
                bias[at : at + rows, k * width : (k + 1) * width] = line

    head_of = lax.broadcasted_iota(jnp.int32, (half, width), 1) // head_dim

    def attend(i, carry):
        logits = scores[i] + bias[...]
        weights = jnp.exp(logits - jnp.max(logits, axis=-1, keepdims=True))
        weights = weights * (1.0 / jnp.sum(weights, axis=-1, keepdims=True))
        mixed_values = jnp.dot(
            weights.astype(jnp.bfloat16), kept[i, :, width:], preferred_element_type=jnp.float32
        )
        taken = jnp.zeros((half, width), jnp.float32)
        for h in range(heads):
            taken = jnp.where(head_of == h, mixed_values[h * half : (h + 1) * half], taken)
        attended[i] = (taken * att_gate[i]).astype(jnp.bfloat16)
        return carry

    lax.fori_loop(0, rows, attend, 0, unroll=2)
    first_ref[...] = pair_ref[:, pl.ds(pl.multiple_of(core * half, 16), half)].astype(
        jnp.float32
    ) + jnp.dot(
        attended[...].reshape(rows * half, width),
        both_out[...].reshape(width, width),
        preferred_element_type=jnp.float32,
    ).reshape(rows, half, width)

    first = first_ref[...].reshape(rows * half, width)
    mixed = norm(first).astype(jnp.bfloat16)
    quad = jnp.dot(mixed, mult_in_ref[...], preferred_element_type=jnp.float32)
    shape = (rows, half, width)
    here_row = z * rows + lax.broadcasted_iota(jnp.int32, shape, 0)
    here_col = (x * n_sub + core) * half + lax.broadcasted_iota(jnp.int32, shape, 1)
    valid = ((here_row < length) & (here_col < length)).astype(jnp.float32)
    a, b, c, d = [quad[:, k * width : (k + 1) * width].reshape(shape) for k in range(4)]
    left[...] = (valid * jax.nn.sigmoid(b) * a).astype(jnp.bfloat16).astype(jnp.float32)
    gathered[z] = (valid * jax.nn.sigmoid(d) * c).astype(jnp.bfloat16)
    gate[...] = jax.nn.sigmoid(
        jnp.dot(mixed, mult_gate_ref[...], preferred_element_type=jnp.float32)
    )

    def source(way, step):
        return lax.rem(z + (n_row - step if way == 0 else step), n_row)

    def ring_copy(way, step, chunk, arrives):
        block = gathered.at[source(way, step), pl.ds(chunk * piece, piece)]
        return pltpu.make_async_remote_copy(
            src_ref=block,
            dst_ref=block,
            send_sem=ring_send.at[way, lax.rem(step, 2), chunk],
            recv_sem=ring_recv.at[way, step - 1 if arrives else step, chunk],
            device_id={"row": up if way == 0 else down},
            device_id_type=MESH,
        )

    def hop(way, step, chunk):
        return ring_copy(way, step, chunk, False)

    def arrival(way, step, chunk):
        return ring_copy(way, step, chunk, True)

    def multiply(owner, chunk, lane):
        for jj in range(piece):
            j = chunk * piece + jj
            right = gathered[owner, j].astype(jnp.float32)
            for i in range(rows):
                stage_f32[lane, pl.ds(i * rows + j, 1)] = jnp.sum(
                    left[i] * right, axis=0, keepdims=True
                )

    def give(block, lane):
        stage[block] = stage_f32[lane].astype(jnp.bfloat16)
        to_owner(block, *part_way)

    for chunk in range(CHUNKS):
        for way in range(2):
            hop(way, 0, chunk).start()

    def own(chunk, carry):
        multiply(z, chunk, 0)
        return carry

    lax.fori_loop(0, CHUNKS, own, 0)
    give(z, 0)

    def visit(n, carry):
        step = lax.div(n, CHUNKS) + 1
        chunk = lax.rem(n, CHUNKS)
        for way in range(2):
            arrival(way, step, chunk).wait_recv()
            last = chunk < CHUNKS // 2 if way == 0 else chunk >= CHUNKS // 2

            @pl.when(step >= 2)
            def _():
                hop(way, step, chunk).wait_send()

            @pl.when(jnp.logical_or(step < far - 1, last))
            def _():
                hop(way, step, chunk).start()

        for way in range(2):
            multiply(source(way, step), chunk, way)

        @pl.when(chunk == CHUNKS - 1)
        def _():
            for way in range(2):
                give(source(way, step), way)

        return carry

    lax.fori_loop(0, (far - 1) * CHUNKS, visit, 0)

    for chunk in range(CHUNKS):
        arrival(0 if chunk < CHUNKS // 2 else 1, far, chunk).wait_recv()
        multiply(source(0, far), chunk, 0)
    give(source(0, far), 0)

    for way in range(2):
        for chunk in range(CHUNKS):
            hop(way, far - 2, chunk).wait_send()
            if (chunk < CHUNKS // 2) == (way == 0):
                hop(way, far - 1, chunk).wait_send()

    for stop in range(2 * ups):
        for k, offset in hops_of(stop):
            bias_hop(stop, k, block_of(stop), offset).wait_send()
    for k in range(2):
        weight_copy(k).wait_send()
    for way in range(2):
        for chunk in range(2):
            x_copy(way, 0, chunk, False).wait_send()
        x_copy(way, 1, way, False).wait_send()

    def sent(block, carry):
        @pl.when(lax.div(block, per_owner) != me)
        def _():
            owner_copy(block, *bias_way).wait_send()
            owner_copy(block, *part_way).wait_send()

        return carry

    lax.fori_loop(0, n_row, sent, 0)

    for slot in range(per_owner):
        total_f32 = None
        for giver in range(owners):
            pltpu.make_async_copy(
                stage.at[0], parts.at[giver, slot], part_recv.at[giver, slot]
            ).wait()
            part = parts[giver, slot].astype(jnp.float32)
            total_f32 = part if total_f32 is None else total_f32 + part
        for i in range(rows):
            tri[i, slot * rows : (slot + 1) * rows] = total_f32[i * rows : (i + 1) * rows]

    tri_normed = norm(tri[...].reshape(rows * half, width)).astype(jnp.bfloat16)
    second = first_ref[...].reshape(rows * half, width) + gate[...] * jnp.dot(
        tri_normed, mult_out_ref[...], preferred_element_type=jnp.float32
    )
    last_normed = norm(second).astype(jnp.bfloat16)
    hidden = jax.nn.relu(
        jnp.dot(last_normed, trans_up_ref[...], preferred_element_type=jnp.float32)
    ).astype(jnp.bfloat16)
    result = second + jnp.dot(hidden, trans_down_ref[...], preferred_element_type=jnp.float32)
    out_ref[...] = result.astype(jnp.bfloat16).reshape(rows, half, width)


def local(
    pair,
    length,
    chain,
    att_proj,
    att_bias,
    chain_bias,
    att_out,
    mult_in,
    mult_gate,
    mult_out,
    trans_up,
    trans_down,
):
    rows, cols, width = pair.shape
    n_row, n_col, n_sub = (lax.axis_size(a) for a in ("row", "col", "sub"))
    owners = n_col * n_sub
    per_owner = n_row // owners
    half = cols // n_sub
    total = rows * n_row
    heads_here = att_bias.shape[1]
    heads = heads_here * n_sub
    spread = att_out.shape[0]
    chain_cols = jnp.pad(
        lax.dynamic_slice_in_dim(chain, lax.axis_index("col") * cols, cols, 0), (0, width - cols)
    )[None]
    bias_w = jnp.pad(att_bias.T, ((0, 8 - heads_here), (0, 0)))
    att_w = lax.dynamic_update_slice_in_dim(
        jnp.zeros((width, 4, spread * n_sub), jnp.bfloat16),
        att_proj,
        lax.axis_index("sub") * spread,
        2,
    ).reshape(width, 4 * spread * n_sub)
    vmem = pl.BlockSpec(memory_space=pltpu.VMEM)
    smem = pl.BlockSpec(memory_space=pltpu.SMEM)
    dma = pltpu.SemaphoreType.DMA
    bf16, f32 = jnp.bfloat16, jnp.float32
    return pl.pallas_call(
        functools.partial(pair_kernel, n_row, n_col, n_sub),
        out_shape=jax.ShapeDtypeStruct((rows, half, width), bf16),
        in_specs=[smem] * 3 + [vmem] * 10,
        out_specs=vmem,
        scratch_shapes=[
            pltpu.VMEM((n_col, rows, cols, width), bf16),
            pltpu.VMEM((rows, total, 2 * width), bf16),
            pltpu.VMEM((rows, heads * half, width), bf16),
            pltpu.VMEM((rows, half, width), f32),
            pltpu.VMEM((rows, heads * half, total), f32),
            pltpu.VMEM((heads * half, total), f32),
            pltpu.VMEM((n_row, heads_here * rows, width), f32),
            pltpu.VMEM((owners, per_owner, heads_here * rows, width), f32),
            pltpu.VMEM(att_w.shape, bf16),
            pltpu.VMEM((n_sub, spread, width), bf16),
            pltpu.VMEM((rows, half, width), bf16),
            pltpu.VMEM((rows, half, width), f32),
            pltpu.VMEM((n_row, rows, half, width), bf16),
            pltpu.VMEM((rows, half, width), f32),
            pltpu.VMEM((2, rows * rows, width), f32),
            pltpu.VMEM((n_row, rows * rows, width), bf16),
            pltpu.VMEM((owners, per_owner, rows * rows, width), bf16),
            pltpu.VMEM((rows, half, width), f32),
            pltpu.VMEM((rows * half, width), f32),
            dma((2, 2, 2)),
            dma((2, 2, 2)),
            dma((2,)),
            dma((2,)),
            dma((n_row // STRIDE, len(LOCAL) + 2)),
            dma((n_row,)),
            dma((n_row,)),
            dma((owners, per_owner)),
            dma((2, 2, CHUNKS)),
            dma((2, n_row // 2, CHUNKS)),
            dma((n_row,)),
            dma((owners, per_owner)),
        ],
        compiler_params=pltpu.CompilerParams(collective_id=0, has_side_effects=True),
    )(
        length,
        chain,
        chain_bias,
        pair,
        chain_cols,
        bias_w,
        att_w,
        att_out,
        mult_in,
        mult_gate,
        mult_out,
        trans_up,
        trans_down,
    )


def solution(mesh):
    placed = (
        P(("grp", "row"), "col", None),
        P("grp"),
        P("grp"),
        P(None, None, "sub"),
        P(None, "sub"),
        P("sub"),
        P("sub", None),
        P(),
        P(),
        P(),
        P(),
        P(),
    )
    return jax.shard_map(
        local,
        mesh=mesh,
        in_specs=placed,
        out_specs=P(("grp", "row"), ("col", "sub"), None),
        check_vma=False,
    )
```

time: 238 us -> 166 us (0.70)
  the two profiles are of different devices: /device:TPU:36 before, /device:TPU:44 now
where the time goes in v2:
time: 166 us
  Pallas kernels  155 us (93%)
  local copies, waits for them, and re-layouts  9.8 us (6%)
    pallas_call x1, Pallas kernels, local(): pl.pallas_call(functools.partial(pair_kernel, n_row, n_col, n_sub), out_s...  155 us
    dynamic_update_slice x1, local copies, waits for them, and re-layouts, local(): lax.dynamic_update_slice_in_dim(jnp.zeros((width, 4, spread * n_sub), jnp...  4.03 us
    unnamed x5, local copies, waits for them, and re-layouts  3.88 us

profile of v2, /device:TPU:44, one launch (start us, length us, event | category | flops | bytes accessed | tf_op | source)
XLA Modules:
  0.0 165.7 jit_solution(4404552371866281077)
XLA Ops:
  0.0 1.0 copy.13
  1.0 4.0 %dynamic_update_slice.3 = bf16[128,4,128]{2,1,0:T(4,128)(2,1)S(1)} dynamic-update-slice(bf16[128,4,128]{2,1,0:T(4,128)(2,1)S(1)} %broadcast_in_dim.7, bf16[128,4,64]{2,1,0:T(4,128)(2,1)S(1)} %copy.13, s32[]{:T(128)} %constant.6.clone.1, s32[]{:T(128)} %constant.6.clone.1, s32[]{:T(128)S(6)} %select_n.7) | dynamic-update-slice | bytes 131076 | tf_op jit(solution)/shard_map/dynamic_update_slice | solution.py:517
  5.1 0.7 copy.16
  5.7 0.8 dynamic_slice.3
  6.5 0.5 pad_bitcast_fusion.chain_cols_ref
  7.0 0.0 copy-start
  7.0 0.7 copy-done
  7.7 0.6 pad.9.bias_w_ref
  8.9 155.2 %shard_map.118 = bf16[12,48,128]{2,1,0:T(8,128)(2,1)} custom-call(s32[1]{0:T(128)S(6)} %copy.19.length_ref, s32[384]{0:T(512)} %chain_ref.1, f32[2]{0:T(128)} %chain_bias_ref.1, bf16[12,96,128]{2,1,0:T(8,128)(2,1)} %pair_ref.1, s32[1,128]{1,0:T(1,128)} %pad_bitcast_fusion.chain_cols_ref, bf16[8,128]{1,0:T(8,128)(2,1)} %pad.9.bias_w_ref, ...), custom_call_target="tpu_custom_call" | custom-call | tf_op jit(solution)/shard_map/pallas_call | solution.py:527
  164.1 1.6 copy.20
  (1 shorter events, 0.0 us)
Async XLA Ops:
  7.0 0.7 copy-start

commit v3 on v2

--- a/solution.py
+++ b/solution.py
@@ -28,8 +28,8 @@
     chain_ref,
     chain_bias_ref,
     pair_ref,
-    chain_cols_ref,
-    bias_w_ref,
+    chain_lanes_ref,
+    att_bias_ref,
     att_w_ref,
     att_out_ref,
     mult_in_ref,
@@ -46,7 +46,7 @@
     bias,
     pieces,
     bias_in,
-    other_w,
+    both_w,
     both_out,
     attended,
     first_ref,
@@ -109,29 +109,37 @@
 
     normed[x] = norm(pair_ref[...].astype(jnp.float32)).astype(jnp.bfloat16)
     both_out[core] = att_out_ref[...]
-
-    lane = lax.broadcasted_iota(jnp.int32, (8, width), 1)
-    line = lax.broadcasted_iota(jnp.int32, (8, width), 0)
-    chain_bias = jnp.zeros((8, width), jnp.float32)
-    for h in range(heads_here):
-        chain_bias = jnp.where(line == h, chain_bias_ref[h], chain_bias)
-    key_valid = ((x * cols + lane) < length).astype(jnp.float32)
+    both_w[core] = att_w_ref[...]
+
+    lane = lax.broadcasted_iota(jnp.int32, (1, width), 1)
+    begin = x * cols
+    turn = lax.rem(begin, width)
+    key = begin + lax.rem(lane + (width - turn), width)
+    key_chain = jnp.zeros((1, width), jnp.int32)
+    for k in range(total // width):
+        held = chain_lanes_ref[:, k * width : (k + 1) * width]
+        key_chain = jnp.where(key // width == k, held, key_chain)
+    key_bias = ((key < length).astype(jnp.float32) - 1.0) * 1000000000.0
     padding = jnp.zeros((width - cols, width), jnp.bfloat16)
+    bias_w = att_bias_ref[...]
     for i in range(rows):
         keys_i = jnp.concatenate([normed[x, i], padding], axis=0)
         term = lax.dot_general(
-            bias_w_ref[...], keys_i, (((1,), (1,)), ((), ())), preferred_element_type=jnp.float32
-        )
-        same = (chain_cols_ref[...] == chain_ref[z * rows + i]).astype(jnp.float32)
-        term = term + chain_bias * same + (key_valid - 1.0) * 1000000000.0
-        term = pltpu.roll(term, lax.rem(x * cols, width), 1)
+            bias_w, keys_i, (((1,), (1,)), ((), ())), preferred_element_type=jnp.float32
+        )
+        term = pltpu.roll(term, turn, 1)
+        same = (key_chain == chain_ref[z * rows + i]).astype(jnp.float32)
         for h in range(heads_here):
-            pieces[z, h * rows + i : h * rows + i + 1] = term[h : h + 1]
+            at = h * rows + i
+            pieces[z, at : at + 1] = term[h : h + 1] + chain_bias_ref[h] * same + key_bias
 
     pl.semaphore_wait(barrier, len(near) + owners - 1)
 
     def weight_copy(k):
-        source, target = [(att_w_ref, other_w), (both_out.at[core], both_out.at[core])][k]
+        source, target = [
+            (att_w_ref, both_w.at[core]),
+            (att_out_ref, both_out.at[core]),
+        ][k]
         return pltpu.make_async_remote_copy(
             src_ref=source,
             dst_ref=target,
@@ -223,11 +231,7 @@
 
     def project(source, chunk):
         tile = normed[source, pl.ds(chunk * block_rows, block_rows)]
-        made = jnp.dot(
-            tile.reshape(block_rows * cols, width),
-            w_all[:, width : 3 * width],
-            preferred_element_type=jnp.float32,
-        ).astype(jnp.bfloat16)
+        made = times(tile.reshape(block_rows * cols, width), w_kept).astype(jnp.bfloat16)
         kept[
             pl.ds(chunk * block_rows, block_rows), pl.ds(pl.multiple_of(source * cols, 32), cols)
         ] = made.reshape(block_rows, cols, 2 * width)
@@ -250,19 +254,25 @@
 
     for k in range(2):
         weight_copy(k).wait_recv()
-    w_all = att_w_ref[...] + other_w[...]
+
+    def joined(g):
+        return jnp.concatenate([both_w[k, g] for k in range(n_sub)], axis=0)
+
+    def times(value, weight):
+        return lax.dot_general(
+            value, weight, (((1,), (1,)), ((), ())), preferred_element_type=jnp.float32
+        )
+
+    w_query, w_gate = joined(0), joined(3)
+    w_kept = jnp.concatenate([joined(1), joined(2)], axis=0)
     tile = normed[x, :, pl.ds(pl.multiple_of(core * half, 16), half)].reshape(rows * half, width)
-    query = (
-        jnp.dot(tile, w_all[:, :width], preferred_element_type=jnp.float32) * head_dim ** (-0.5)
-    ).astype(jnp.bfloat16)
+    query = (times(tile, w_query) * head_dim ** (-0.5)).astype(jnp.bfloat16)
     head_of = lax.broadcasted_iota(jnp.int32, (rows * half, width), 1) // head_dim
     for h in range(heads):
         queries[:, h * half : (h + 1) * half] = jnp.where(
             head_of == h, query, jnp.zeros_like(query)
         ).reshape(rows, half, width)
-    att_gate[...] = jax.nn.sigmoid(
-        jnp.dot(tile, w_all[:, 3 * width :], preferred_element_type=jnp.float32)
-    ).reshape(rows, half, width)
+    att_gate[...] = jax.nn.sigmoid(times(tile, w_gate)).reshape(rows, half, width)
     for chunk in range(2):
         project(x, chunk)
 
@@ -510,16 +520,6 @@
     heads_here = att_bias.shape[1]
     heads = heads_here * n_sub
     spread = att_out.shape[0]
-    chain_cols = jnp.pad(
-        lax.dynamic_slice_in_dim(chain, lax.axis_index("col") * cols, cols, 0), (0, width - cols)
-    )[None]
-    bias_w = jnp.pad(att_bias.T, ((0, 8 - heads_here), (0, 0)))
-    att_w = lax.dynamic_update_slice_in_dim(
-        jnp.zeros((width, 4, spread * n_sub), jnp.bfloat16),
-        att_proj,
-        lax.axis_index("sub") * spread,
-        2,
-    ).reshape(width, 4 * spread * n_sub)
     vmem = pl.BlockSpec(memory_space=pltpu.VMEM)
     smem = pl.BlockSpec(memory_space=pltpu.SMEM)
     dma = pltpu.SemaphoreType.DMA
@@ -538,7 +538,7 @@
             pltpu.VMEM((heads * half, total), f32),
             pltpu.VMEM((n_row, heads_here * rows, width), f32),
             pltpu.VMEM((owners, per_owner, heads_here * rows, width), f32),
-            pltpu.VMEM(att_w.shape, bf16),
+            pltpu.VMEM((n_sub, 4, spread, width), bf16),
             pltpu.VMEM((n_sub, spread, width), bf16),
             pltpu.VMEM((rows, half, width), bf16),
             pltpu.VMEM((rows, half, width), f32),
@@ -568,9 +568,9 @@
         chain,
         chain_bias,
         pair,
-        chain_cols,
-        bias_w,
-        att_w,
+        chain[None],
+        att_bias.T,
+        att_proj.transpose(1, 2, 0),
         att_out,
         mult_in,
         mult_gate,

time: 166 us -> 145 us (0.87)
  Pallas kernels: 155 us -> 141 us
  local copies, waits for them, and re-layouts: 9.8 us -> 2.82 us
    pallas_call x1, Pallas kernels: 155 us -> 141 us  [local(): pl.pallas_call(functools.partial(pair_kernel, n_row, n_col, n_sub), out_s...]
    dynamic_update_slice x1 -> x0, local copies, waits for them, and re-layouts: 4.03 us -> none  [local(): lax.dynamic_update_slice_in_dim(jnp.zeros((width, 4, spread * n_sub), jnp...]
    unnamed x5 -> x3, local copies, waits for them, and re-layouts: 3.88 us -> 2.26 us
where the time goes in v3:
time: 145 us
  Pallas kernels  141 us (97%)
  local copies, waits for them, and re-layouts  2.82 us (2%)
    pallas_call x1, Pallas kernels, local(): pl.pallas_call(functools.partial(pair_kernel, n_row, n_col, n_sub), out_s...  141 us

profile of v3, /device:TPU:44, one launch (start us, length us, event | category | flops | bytes accessed | tf_op | source)
XLA Modules:
  0.0 144.9 jit_solution(14091897019484500175)
XLA Ops:
  0.7 0.0 copy-start
  0.7 0.7 copy-done
  1.3 0.6 broadcast_in_dim.3.chain_lanes_ref
  1.9 141.4 %shard_map.118 = bf16[12,48,128]{2,1,0:T(8,128)(2,1)} custom-call(s32[1]{0:T(128)S(6)} %copy.14.length_ref, s32[384]{0:T(512)} %chain_ref.1, f32[2]{0:T(128)} %chain_bias_ref.1, bf16[12,96,128]{2,1,0:T(8,128)(2,1)} %pair_ref.1, s32[1,384]{1,0:T(1,128)} %broadcast_in_dim.3.chain_lanes_ref, bf16[2,128]{1,0:T(2,128)(2,1)} %bitcast.3, ...), custom_call_target="tpu_custom_call" | custom-call | tf_op jit(solution)/shard_map/pallas_call | solution.py:527
  143.3 1.6 %copy.15 = bf16[12,48,128]{2,1,0:T(8,128)(2,1)} copy(bf16[12,48,128]{2,1,0:T(8,128)(2,1)} %shard_map.118) | data formatting | bytes 294912
Async XLA Ops:
  0.7 0.7 copy-start

commit v4 on v3

--- a/solution.py
+++ b/solution.py
@@ -10,7 +10,6 @@
 MESH = pl.DeviceIdType.MESH
 CHUNKS = 4
 STRIDE = 4
-LOCAL = (-1, 1, 2)
 
 
 def norm(value):
@@ -62,6 +61,7 @@
     weight_send,
     weight_recv,
     chain_send,
+    direct_send,
     chain_recv,
     bias_send,
     bias_recv,
@@ -89,15 +89,26 @@
     down = lax.rem(z + n_row - 1, n_row)
     length = length_ref[0]
 
-    def row_at(offset):
-        return lax.rem(z + (offset + n_row), n_row)
+    def greet(other):
+        pl.semaphore_signal(barrier, inc=1, device_id={"row": other}, device_id_type=MESH)
 
     barrier = pltpu.get_barrier_semaphore()
-    near = (1, -1, 2, -2, STRIDE, -STRIDE)
-    for offset in near:
-        pl.semaphore_signal(
-            barrier, inc=1, device_id={"row": row_at(offset)}, device_id_type=MESH
-        )
+    for offset in range(1, STRIDE + 1):
+
+        @pl.when(z >= offset)
+        def _():
+            greet(z - offset)
+
+    def greet_later(other, carry):
+        greet(other)
+        return carry
+
+    lax.fori_loop(z + 1, n_row, greet_later, 0)
+
+    @pl.when(z == n_row - 1)
+    def _():
+        greet(0)
+
     for step in range(1, owners):
         other = lax.rem(me + step, owners)
         pl.semaphore_signal(
@@ -117,7 +128,7 @@
     key = begin + lax.rem(lane + (width - turn), width)
     key_chain = jnp.zeros((1, width), jnp.int32)
     for k in range(total // width):
-        held = chain_lanes_ref[:, k * width : (k + 1) * width]
+        held = chain_lanes_ref[k * width : (k + 1) * width].reshape(1, width)
         key_chain = jnp.where(key // width == k, held, key_chain)
     key_bias = ((key < length).astype(jnp.float32) - 1.0) * 1000000000.0
     padding = jnp.zeros((width - cols, width), jnp.bfloat16)
@@ -133,7 +144,9 @@
             at = h * rows + i
             pieces[z, at : at + 1] = term[h : h + 1] + chain_bias_ref[h] * same + key_bias
 
-    pl.semaphore_wait(barrier, len(near) + owners - 1)
+    ends = jnp.where(z == 0, 1, 0)
+    after = jnp.minimum(n_row - 1 - z, STRIDE)
+    pl.semaphore_wait(barrier, z + after + ends + owners - 1)
 
     def weight_copy(k):
         source, target = [
@@ -162,15 +175,30 @@
             device_id_type=MESH,
         )
 
-    def bias_hop(stop, k, block, offset):
+    def bias_hop(block, target, send_sem):
         return pltpu.make_async_remote_copy(
             src_ref=pieces.at[block],
             dst_ref=pieces.at[block],
-            send_sem=chain_send.at[stop, k],
+            send_sem=send_sem,
             recv_sem=chain_recv.at[block],
-            device_id={"row": row_at(offset)},
+            device_id={"row": target},
             device_id_type=MESH,
         )
+
+    def direct(target):
+        return bias_hop(z, target, direct_send.at[target])
+
+    def relay(block, offset):
+        return bias_hop(
+            block, z + offset, chain_send.at[lax.div(block, STRIDE), offset - 1]
+        )
+
+    def each_relay(block, act):
+        for offset in range(STRIDE, 0, -1):
+
+            @pl.when(z + offset < n_row)
+            def _():
+                act(relay(block, offset))
 
     def owner_copy(block, source, target, send_sem, recv_sem):
         dest = lax.div(block, per_owner)
@@ -199,35 +227,40 @@
 
     bias_way = (pieces, bias_in, bias_send, bias_recv)
     part_way = (stage, parts, part_send, part_recv)
-    ups = n_row // (2 * STRIDE)
-
-    def hops_of(stop):
-        if stop == 0:
-            ahead = [(0, STRIDE), (len(LOCAL) + 1, -STRIDE)]
-        elif stop < ups:
-            ahead = [(0, STRIDE)]
-        elif stop == ups or stop == 2 * ups - 1:
-            ahead = []
-        else:
-            ahead = [(0, -STRIDE)]
-        return ahead + [(1 + n, offset) for n, offset in enumerate(LOCAL)]
-
-    def block_of(stop):
-        return row_at(-STRIDE * stop if stop <= ups else STRIDE * (stop - ups))
-
-    def pass_on(stop):
-        block = block_of(stop)
-        if stop > 0:
-            bias_hop(stop, 0, block, 0).wait_recv()
-        for k, offset in hops_of(stop):
-            bias_hop(stop, k, block, offset).start()
+
+    def own_bias():
+        each_relay(z, lambda copy: copy.start())
+
+        def send(n, carry):
+            distance = far - n
+
+            @pl.when(z >= distance)
+            def _():
+                direct(z - distance).start()
+
+            @pl.when(jnp.logical_and(z + distance >= n_row, distance < far))
+            def _():
+                direct(z + distance - n_row).start()
+
+            return carry
+
+        lax.fori_loop(0, far, send, 0)
+        to_owner(z, *bias_way)
+
+    def take_earlier(block, carry):
+        bias_hop(block, z, chain_send.at[0, 0]).wait_recv()
+
+        @pl.when(lax.rem(z - block, STRIDE) == 0)
+        def _():
+            each_relay(block, lambda copy: copy.start())
+
         to_owner(block, *bias_way)
-
-    def take_local(stop):
-        for offset in LOCAL:
-            block = lax.rem(block_of(stop) + (n_row - offset), n_row)
-            bias_hop(stop, 0, block, 0).wait_recv()
-            to_owner(block, *bias_way)
+        return carry
+
+    def take_later(block, carry):
+        bias_hop(block, z, chain_send.at[0, 0]).wait_recv()
+        to_owner(block, *bias_way)
+        return carry
 
     def project(source, chunk):
         tile = normed[source, pl.ds(chunk * block_rows, block_rows)]
@@ -245,7 +278,7 @@
         )
         return carry
 
-    pass_on(0)
+    own_bias()
     for k in range(2):
         weight_copy(k).start()
     for chunk in range(2):
@@ -280,36 +313,24 @@
     x_down = lax.rem(x + 1, n_col)
     x_far = lax.rem(x + 2, n_col)
 
-    def stage_of(step):
-        if step <= ups:
-            pass_on(step)
-        if step < ups:
-            pass_on(ups + step)
-        take_local(step - 1)
-        if 1 <= step - 1 < ups:
-            take_local(ups + step - 1)
-
-    stage_of(1)
     x_copy(0, 0, 0, True).wait_recv()
     x_copy(0, 1, 0, False).start()
     x_copy(1, 0, 1, True).wait_recv()
     x_copy(1, 1, 1, False).start()
     project(x_up, 0)
     project(x_down, 1)
-    stage_of(2)
+    lax.fori_loop(0, z, take_earlier, 0)
     x_copy(0, 0, 1, True).wait_recv()
     project(x_up, 1)
     x_copy(1, 0, 0, True).wait_recv()
     project(x_down, 0)
-    stage_of(3)
     x_copy(0, 1, 0, True).wait_recv()
     project(x_far, 0)
     lax.fori_loop(0, block_rows, score, 0)
-    stage_of(4)
     x_copy(1, 1, 1, True).wait_recv()
     project(x_far, 1)
     lax.fori_loop(block_rows, rows, score, 0)
-    take_local(ups)
+    lax.fori_loop(z + 1, n_row, take_later, 0)
 
     for slot in range(per_owner):
         for giver in range(owners):
@@ -454,9 +475,20 @@
             if (chunk < CHUNKS // 2) == (way == 0):
                 hop(way, far - 1, chunk).wait_send()
 
-    for stop in range(2 * ups):
-        for k, offset in hops_of(stop):
-            bias_hop(stop, k, block_of(stop), offset).wait_send()
+    def told(block, carry):
+        @pl.when(lax.rem(z - block, STRIDE) == 0)
+        def _():
+            each_relay(block, lambda copy: copy.wait_send())
+
+        return carry
+
+    lax.fori_loop(0, z + 1, told, 0)
+
+    def reached(target, carry):
+        direct(target).wait_send()
+        return carry
+
+    lax.fori_loop(0, z, reached, 0)
     for k in range(2):
         weight_copy(k).wait_send()
     for way in range(2):
@@ -553,7 +585,8 @@
             dma((2, 2, 2)),
             dma((2,)),
             dma((2,)),
-            dma((n_row // STRIDE, len(LOCAL) + 2)),
+            dma((n_row // STRIDE, STRIDE)),
+            dma((n_row,)),
             dma((n_row,)),
             dma((n_row,)),
             dma((owners, per_owner)),
@@ -568,7 +601,7 @@
         chain,
         chain_bias,
         pair,
-        chain[None],
+        chain,
         att_bias.T,
         att_proj.transpose(1, 2, 0),
         att_out,

time: 145 us -> 216 us (1.49)
  Pallas kernels: 141 us -> 213 us
    pallas_call x1, Pallas kernels: 141 us -> 213 us  [local(): pl.pallas_call(functools.partial(pair_kernel, n_row, n_col, n_sub), out_s...]
where the time goes in v4:
time: 216 us
  Pallas kernels  213 us (99%)
    pallas_call x1, Pallas kernels, local(): pl.pallas_call(functools.partial(pair_kernel, n_row, n_col, n_sub), out_s...  213 us

profile of v4, /device:TPU:44, one launch (start us, length us, event | category | flops | bytes accessed | tf_op | source)
XLA Modules:
  0.0 215.5 jit_solution(2086074902351864916)
XLA Ops:
  0.7 213.3 %shard_map.118 = bf16[12,48,128]{2,1,0:T(8,128)(2,1)} custom-call(s32[1]{0:T(128)S(6)} %copy.14.length_ref, s32[384]{0:T(512)} %chain_lanes_ref.1, f32[2]{0:T(128)} %chain_bias_ref.1, bf16[12,96,128]{2,1,0:T(8,128)(2,1)} %pair_ref.1, s32[384]{0:T(512)} %chain_lanes_ref.1, bf16[2,128]{1,0:T(2,128)(2,1)} %bitcast.3, bf16[4,64,128]{2,1,0:T(8,128)(2,1)} %bitcast.2, ...), custom_call_target="tpu_custom_call" | custom-call | tf_op jit(solution)/shard_map/pallas_call | solution.py:559
  214.0 1.6 copy.15

commit v5 on v3

v5 whole, which is shorter than its diff:
```python
import functools

import jax
import jax.numpy as jnp
from jax import lax
from jax.experimental import pallas as pl
from jax.experimental.pallas import tpu as pltpu
from jax.sharding import PartitionSpec as P

MESH = pl.DeviceIdType.MESH
LAG = 3
STRIDE = 4


def norm(value):
    mean = jnp.mean(value, axis=-1, keepdims=True)
    centred = value - mean
    variance = jnp.mean(centred * centred, axis=-1, keepdims=True)
    return centred * lax.rsqrt(variance + 1e-05)


def pair_kernel(
    n_row,
    n_col,
    n_sub,
    length_ref,
    chain_ref,
    chain_bias_ref,
    pair_ref,
    chain_lanes_ref,
    att_bias_ref,
    att_w_ref,
    att_out_ref,
    mult_in_ref,
    mult_gate_ref,
    mult_out_ref,
    trans_up_ref,
    trans_down_ref,
    out_ref,
    raws,
    tile_f32,
    mine,
    kept,
    query_f32,
    query_rows,
    att_gate,
    scores,
    bias,
    pieces,
    bias_in,
    both_w,
    both_out,
    att_f32,
    first,
    first_in,
    whole_first,
    gathered,
    left,
    right_f32,
    stage_f32,
    stage,
    parts,
    tri,
    x_send,
    x_recv,
    weight_send,
    weight_recv,
    chain_send,
    chain_recv,
    bias_send,
    bias_recv,
    first_send,
    first_recv,
    ring_send,
    ring_recv,
    part_send,
    part_recv,
):
    rows, cols, width = pair_ref.shape
    half = cols // n_sub
    total = rows * n_row
    block_rows = rows // 2
    area = rows * rows
    heads_here = pieces.shape[1] // rows
    heads = heads_here * n_sub
    head_dim = width // heads
    group = heads * rows
    z = lax.axis_index("row")
    x = lax.axis_index("col")
    core = lax.axis_index("sub")
    owners = n_col * n_sub
    me = x * n_sub + core
    slots = n_row // owners
    far = n_row // 2
    up = lax.rem(z + 1, n_row)
    down = lax.rem(z + n_row - 1, n_row)
    length = length_ref[0]

    def row_at(offset):
        return lax.rem(z + (offset + n_row), n_row)

    def seat(owner):
        return {"col": lax.div(owner, n_sub), "sub": lax.rem(owner, n_sub)}

    barrier = pltpu.get_barrier_semaphore()
    for offset in (STRIDE, -STRIDE):
        pl.semaphore_signal(
            barrier, inc=1, device_id={"row": row_at(offset)}, device_id_type=MESH
        )
    for step in range(1, owners):
        pl.semaphore_signal(
            barrier, inc=1, device_id=seat(lax.rem(me + step, owners)), device_id_type=MESH
        )

    gang, rank = lax.div(z, STRIDE), lax.rem(z, STRIDE)

    def mate(n):
        return gang * STRIDE + lax.rem(rank + n, STRIDE)

    def greet(owner, carry):
        for n in range(1, STRIDE):
            pl.semaphore_signal(
                barrier, inc=1, device_id={"row": mate(n), **seat(owner)}, device_id_type=MESH
            )
        return carry

    lax.fori_loop(0, owners, greet, 0)
    for edge, neighbour in ((0, down), (STRIDE - 1, up)):

        @pl.when(rank == edge)
        def _():
            pl.semaphore_signal(
                barrier, inc=1, device_id={"row": neighbour}, device_id_type=MESH
            )

    raws[x] = pair_ref[...]
    both_out[core] = att_out_ref[...]
    both_w[core] = att_w_ref[...]
    right_f32[...] = jnp.zeros_like(right_f32)

    lane = lax.broadcasted_iota(jnp.int32, (1, width), 1)
    begin = x * cols
    turn = lax.rem(begin, width)
    key = begin + lax.rem(lane + (width - turn), width)
    key_chain = jnp.zeros((1, width), jnp.int32)
    for k in range(total // width):
        held = chain_lanes_ref[k * width : (k + 1) * width].reshape(1, width)
        key_chain = jnp.where(key // width == k, held, key_chain)
    key_bias = ((key < length).astype(jnp.float32) - 1.0) * 1000000000.0
    padding = jnp.zeros((width - cols, width), jnp.bfloat16)
    bias_w = att_bias_ref[...]
    for i in range(rows):
        keys_i = norm(pair_ref[i].astype(jnp.float32)).astype(jnp.bfloat16)
        keys_i = jnp.concatenate([keys_i, padding], axis=0)
        term = lax.dot_general(
            bias_w, keys_i, (((1,), (1,)), ((), ())), preferred_element_type=jnp.float32
        )
        term = pltpu.roll(term, turn, 1)
        same = (key_chain == chain_ref[z * rows + i]).astype(jnp.float32)
        for h in range(heads_here):
            at = h * rows + i
            pieces[z, at : at + 1] = term[h : h + 1] + chain_bias_ref[h] * same + key_bias

    at_edge = jnp.where(jnp.logical_or(rank == 0, rank == STRIDE - 1), 1, 0)
    pl.semaphore_wait(barrier, 2 + owners - 1 + (STRIDE - 1) * owners + at_edge)

    def weight_copy(k):
        source, target = [
            (att_w_ref, both_w.at[core]),
            (att_out_ref, both_out.at[core]),
        ][k]
        return pltpu.make_async_remote_copy(
            src_ref=source,
            dst_ref=target,
            send_sem=weight_send.at[k],
            recv_sem=weight_recv.at[k],
            device_id={"sub": 1 - core},
            device_id_type=MESH,
        )

    def x_copy(way, step, chunk, arrives):
        distance = step + 1 if arrives else step
        source = lax.rem(x + (n_col - distance if way == 0 else distance), n_col)
        block = raws.at[source, pl.ds(chunk * block_rows, block_rows)]
        return pltpu.make_async_remote_copy(
            src_ref=block,
            dst_ref=block,
            send_sem=x_send.at[way, step, chunk],
            recv_sem=x_recv.at[way, step, chunk],
            device_id={"col": lax.rem(x + (1 if way == 0 else n_col - 1), n_col)},
            device_id_type=MESH,
        )

    def bias_hop(block, offset, send_sem):
        return pltpu.make_async_remote_copy(
            src_ref=pieces.at[block],
            dst_ref=pieces.at[block],
            send_sem=send_sem,
            recv_sem=chain_recv.at[block],
            device_id={"row": row_at(offset)},
            device_id_type=MESH,
        )

    def bias_copy(block, stop, n):
        owner, slot = lax.rem(block, owners), lax.div(block, owners)
        return pltpu.make_async_remote_copy(
            src_ref=pieces.at[block],
            dst_ref=bias_in.at[me, slot],
            send_sem=bias_send.at[stop, n],
            recv_sem=bias_recv.at[me, slot],
            device_id={"row": mate(n), **seat(owner)},
            device_id_type=MESH,
        )

    def deliver(block, stop):
        slot = lax.div(block, owners)
        own = lax.rem(block, owners) == me
        for n in range(1, STRIDE):
            bias_copy(block, stop, n).start()

        @pl.when(own)
        def _():
            pltpu.make_async_copy(
                pieces.at[block], bias_in.at[me, slot], bias_recv.at[me, slot]
            ).start()

        @pl.when(jnp.logical_not(own))
        def _():
            bias_copy(block, stop, 0).start()

    gangs = n_row // STRIDE
    reach = gangs // 2
    nearer_downs = jnp.minimum(gangs - 1 - gang, reach)

    def turn_of(position):
        is_down = jnp.logical_and(position >= gang, position < gang + nearer_downs)
        hops = jnp.where(
            position < gang,
            position + 1,
            jnp.where(is_down, position - gang + 1, position - nearer_downs + 1),
        )
        origin = lax.rem(gang + gangs + jnp.where(is_down, hops, -hops), gangs)
        downs = jnp.minimum(origin, reach)
        goes_down = jnp.logical_and(is_down, hops < downs)
        goes_up = jnp.logical_and(jnp.logical_not(is_down), hops < gangs - 1 - downs)
        return origin * STRIDE + rank, goes_up, goes_down

    def pass_on(position, carry):
        block, goes_up, goes_down = turn_of(position)
        bias_hop(block, 0, chain_send.at[0, 0]).wait_recv()

        @pl.when(goes_up)
        def _():
            bias_hop(block, STRIDE, chain_send.at[position + 1, 0]).start()

        @pl.when(goes_down)
        def _():
            bias_hop(block, -STRIDE, chain_send.at[position + 1, 0]).start()

        deliver(block, position + 1)
        return carry

    def w_of(g):
        return jnp.concatenate([both_w[k, g] for k in range(n_sub)], axis=0)

    def times(value, weight):
        return lax.dot_general(
            value, weight, (((1,), (1,)), ((), ())), preferred_element_type=jnp.float32
        )

    def project(source, chunk):
        tile = raws[source, pl.ds(chunk * block_rows, block_rows)].astype(jnp.float32)
        tile_f32[...] = tile
        flat = norm(tile).astype(jnp.bfloat16).reshape(block_rows * cols, width)
        made = times(flat, w_kept).astype(jnp.bfloat16)
        kept[
            pl.ds(chunk * block_rows, block_rows), pl.ds(pl.multiple_of(source * cols, 32), cols)
        ] = made.reshape(block_rows, cols, 2 * width)
        for i in range(block_rows):
            mine[source, pl.ds(chunk * block_rows + i, rows, stride=rows)] = tile_f32[
                i, pl.ds(me * rows, rows)
            ]

    bias_hop(z, STRIDE, chain_send.at[0, 0]).start()

    @pl.when(gang > 0)
    def _():
        bias_hop(z, -STRIDE, chain_send.at[0, 1]).start()

    deliver(z, 0)
    for k in range(2):
        weight_copy(k).start()
    for chunk in range(2):
        for way in range(2):
            x_copy(way, 0, chunk if way == 0 else 1 - chunk, False).start()

    lax.fori_loop(0, gang, pass_on, 0)
    for k in range(2):
        weight_copy(k).wait_recv()
    w_query, w_gate = w_of(0), w_of(3)
    w_kept = jnp.concatenate([w_of(1), w_of(2)], axis=0)
    for chunk in range(2):
        project(x, chunk)

    x_up = lax.rem(x + n_col - 1, n_col)
    x_down = lax.rem(x + 1, n_col)
    x_far = lax.rem(x + 2, n_col)
    x_copy(0, 0, 0, True).wait_recv()
    x_copy(0, 1, 0, False).start()
    x_copy(1, 0, 1, True).wait_recv()
    x_copy(1, 1, 1, False).start()
    project(x_up, 0)
    project(x_down, 1)
    x_copy(0, 0, 1, True).wait_recv()
    project(x_up, 1)
    x_copy(1, 0, 0, True).wait_recv()
    project(x_down, 0)
    x_copy(0, 1, 0, True).wait_recv()
    project(x_far, 0)
    x_copy(1, 1, 1, True).wait_recv()
    project(x_far, 1)

    lane_head = lax.broadcasted_iota(jnp.int32, (rows, width), 1) // head_dim
    for q in range(slots):
        tile = norm(mine[q]).astype(jnp.bfloat16)
        query_f32[q] = (
            (times(tile, w_query) * head_dim ** (-0.5)).astype(jnp.bfloat16).astype(jnp.float32)
        )
        att_gate[q] = jax.nn.sigmoid(times(tile, w_gate))

    def score(i, carry):
        for q in range(slots):
            line = query_f32[q, pl.ds(i, rows, stride=rows)]
            for h in range(heads):
                at = q * group + h * rows
                query_rows[at : at + rows] = jnp.where(lane_head == h, line, 0.0)
        scores[i] = times(query_rows[...].astype(jnp.bfloat16), kept[i, :, :width])
        return carry

    lax.fori_loop(0, rows, score, 0)
    later = jnp.where(
        gang == reach - 2, 2, jnp.where((gang == 0) | (gang > reach), 0, 1)
    )
    ready = gangs - 1 - later
    lax.fori_loop(gang, ready, pass_on, 0)

    def source(way, step):
        return lax.rem(z + (n_row - step if way == 0 else step), n_row)

    def ring_copy(way, step, chunk, arrives):
        block = gathered.at[source(way, step), chunk]
        return pltpu.make_async_remote_copy(
            src_ref=block,
            dst_ref=block,
            send_sem=ring_send.at[way, lax.rem(step, 2), chunk],
            recv_sem=ring_recv.at[way, step - 1 if arrives else step, chunk],
            device_id={"row": up if way == 0 else down},
            device_id_type=MESH,
        )

    def hop(way, step, chunk):
        return ring_copy(way, step, chunk, False)

    def arrival(way, step, chunk):
        return ring_copy(way, step, chunk, True)

    def part_copy(block):
        dest, slot = lax.div(block, slots), lax.rem(block, slots)
        return pltpu.make_async_remote_copy(
            src_ref=stage.at[block],
            dst_ref=parts.at[me, slot],
            send_sem=part_send.at[block],
            recv_sem=part_recv.at[me, slot],
            device_id=seat(dest),
            device_id_type=MESH,
        )

    def give(block):
        slot = lax.rem(block, slots)
        own = lax.div(block, slots) == me
        stage[block] = stage_f32[block].astype(jnp.bfloat16)

        @pl.when(own)
        def _():
            pltpu.make_async_copy(
                stage.at[block], parts.at[me, slot], part_recv.at[me, slot]
            ).start()

        @pl.when(jnp.logical_not(own))
        def _():
            part_copy(block).start()

    def first_copy(q):
        block = q * owners + me
        dest, slot = lax.div(block, slots), lax.rem(block, slots)
        return pltpu.make_async_remote_copy(
            src_ref=first.at[q],
            dst_ref=first_in.at[slot],
            send_sem=first_send.at[q],
            recv_sem=first_recv.at[slot],
            device_id=seat(dest),
            device_id_type=MESH,
        )

    def first_stays(q):
        return lax.div(q * owners + me, slots) == me

    def multiply(block, q):
        right_f32[:area] = gathered[block, q].astype(jnp.float32)
        for i in range(rows):
            total_i = None
            for k in range(rows):
                term = left[q, k * rows + i : k * rows + i + 1] * right_f32[
                    k * rows : k * rows + 16
                ]
                total_i = term if total_i is None else total_i + term
            stage_f32[block, i * rows : (i + 1) * rows] += total_i[:rows]

    def settle(low, high):
        for q in range(low, high):
            for giver in range(owners):
                pltpu.make_async_copy(
                    pieces.at[0], bias_in.at[giver, q], bias_recv.at[giver, q]
                ).wait()
            for h in range(heads):
                giver, own_head = h // heads_here, h % heads_here
                at = q * group + h * rows
                for k in range(total // width):
                    line = None
                    for tile in range(n_col):
                        start = tile * cols - k * width
                        if start + cols <= 0 or start >= width:
                            continue
                        held = bias_in[
                            tile * n_sub + giver, q, own_head * rows : (own_head + 1) * rows
                        ]
                        line = held if line is None else jnp.where(lane_of >= start, held, line)
                    bias[at : at + rows, k * width : (k + 1) * width] = line

        def attend(i, carry):
            logits = scores[i, low * group : high * group] + bias[low * group : high * group]
            weights = jnp.exp(logits - jnp.max(logits, axis=-1, keepdims=True))
            weights = weights * (1.0 / jnp.sum(weights, axis=-1, keepdims=True))
            made = jnp.dot(
                weights.astype(jnp.bfloat16), kept[i, :, width:], preferred_element_type=jnp.float32
            )
            for q in range(low, high):
                at = (q - low) * group
                taken = made[at : at + rows]
                for h in range(1, heads):
                    other = made[at + h * rows : at + (h + 1) * rows]
                    taken = jnp.where(lane_head == h, other, taken)
                att_f32[q, pl.ds(i, rows, stride=rows)] = taken
            return carry

        lax.fori_loop(0, rows, attend, 0, unroll=2)
        for q in range(low, high):
            attended = (att_f32[q] * att_gate[q]).astype(jnp.bfloat16)
            first_q = mine[q] + jnp.dot(
                attended,
                both_out[...].reshape(width, width),
                preferred_element_type=jnp.float32,
            )
            first[q] = first_q
            quad = jnp.dot(
                norm(first_q).astype(jnp.bfloat16),
                mult_in_ref[...],
                preferred_element_type=jnp.float32,
            )
            index = lax.broadcasted_iota(jnp.int32, (area, width), 0)
            here_row = z * rows + lax.rem(index, rows)
            here_col = (q * owners + me) * rows + lax.div(index, rows)
            valid = ((here_row < length) & (here_col < length)).astype(jnp.float32)
            a, b, c, d = [quad[:, k * width : (k + 1) * width] for k in range(4)]
            left[q] = (valid * jax.nn.sigmoid(b) * a).astype(jnp.bfloat16).astype(jnp.float32)
            gathered[z, q] = (valid * jax.nn.sigmoid(d) * c).astype(jnp.bfloat16)
            for way in range(2):
                hop(way, 0, q).start()
        for q in range(low, high):
            slot = lax.rem(q * owners + me, slots)

            @pl.when(first_stays(q))
            def _():
                pltpu.make_async_copy(first.at[q], first_in.at[slot], first_recv.at[slot]).start()

            @pl.when(jnp.logical_not(first_stays(q)))
            def _():
                first_copy(q).start()

        def own(q, carry):
            multiply(z, q)
            return carry

        lax.fori_loop(low, high, own, 0)

    def visit(step, chunk):
        is_last = [chunk < slots // 2, chunk >= slots // 2]
        present = [
            jnp.logical_or(step < far, jnp.logical_and(step == far, last)) for last in is_last
        ]
        for way in range(2):
            goes = jnp.logical_or(
                step < far - 1, jnp.logical_and(step == far - 1, is_last[way])
            )

            @pl.when(present[way])
            def _():
                arrival(way, step, chunk).wait_recv()

            @pl.when(jnp.logical_and(goes, step >= 2))
            def _():
                hop(way, step, chunk).wait_send()

            @pl.when(goes)
            def _():
                hop(way, step, chunk).start()

        for way in range(2):

            @pl.when(present[way])
            def _():
                block = source(way, step)
                multiply(block, chunk)

                @pl.when(chunk == slots - 1)
                def _():
                    give(block)

    lane_of = lax.broadcasted_iota(jnp.int32, (rows, width), 1)
    stage_f32[...] = jnp.zeros_like(stage_f32)
    early = slots - 1
    settle(0, early)

    late_step = jnp.where(gang == reach - 1, LAG, 1)

    def early_step(step, carry):
        def early_visit(chunk, inner):
            visit(step, chunk)
            return inner

        lax.fori_loop(0, early, early_visit, 0)
        lax.fori_loop(jnp.where(step == late_step, ready, gangs - 1), gangs - 1, pass_on, 0)
        return carry

    lax.fori_loop(1, LAG + 1, early_step, 0)
    settle(early, slots)
    give(z)

    def both_visit(n, carry):
        chunk = lax.rem(n, slots)
        step = LAG + 1 + lax.div(n, slots) - jnp.where(chunk == early, LAG, 0)
        visit(step, chunk)
        return carry

    lax.fori_loop(0, far * slots, both_visit, 0)

    for way in range(2):
        for chunk in range(slots):
            last = far - 1 if (chunk < slots // 2) == (way == 0) else far - 2
            hop(way, last - 1, chunk).wait_send()
            hop(way, last, chunk).wait_send()

    def told(position, carry):
        block, goes_up, goes_down = turn_of(position)

        @pl.when(jnp.logical_or(goes_up, goes_down))
        def _():
            bias_hop(block, STRIDE, chain_send.at[position + 1, 0]).wait_send()

        return carry

    lax.fori_loop(0, gangs - 1, told, 0)
    bias_hop(z, STRIDE, chain_send.at[0, 0]).wait_send()

    @pl.when(gang > 0)
    def _():
        bias_hop(z, -STRIDE, chain_send.at[0, 1]).wait_send()

    def delivered(stop, carry):
        block = jnp.where(stop == 0, z, turn_of(jnp.maximum(stop - 1, 0))[0])
        for n in range(1, STRIDE):
            bias_copy(block, stop, n).wait_send()

        @pl.when(lax.rem(block, owners) != me)
        def _():
            bias_copy(block, stop, 0).wait_send()

        return carry

    lax.fori_loop(0, gangs, delivered, 0)
    for k in range(2):
        weight_copy(k).wait_send()
    for way in range(2):
        for chunk in range(2):
            x_copy(way, 0, chunk, False).wait_send()
        x_copy(way, 1, way, False).wait_send()
    for q in range(slots):

        @pl.when(jnp.logical_not(first_stays(q)))
        def _():
            first_copy(q).wait_send()

    def sent(block, carry):
        @pl.when(lax.div(block, slots) != me)
        def _():
            part_copy(block).wait_send()

        return carry

    lax.fori_loop(0, n_row, sent, 0)

    for slot in range(slots):
        pltpu.make_async_copy(first.at[0], first_in.at[slot], first_recv.at[slot]).wait()
        sum_f32 = None
        for giver in range(owners):
            pltpu.make_async_copy(
                stage.at[0], parts.at[giver, slot], part_recv.at[giver, slot]
            ).wait()
            part = parts[giver, slot].astype(jnp.float32)
            sum_f32 = part if sum_f32 is None else sum_f32 + part
        for i in range(rows):
            tri[i, slot * rows : (slot + 1) * rows] = sum_f32[i * rows : (i + 1) * rows]
            whole_first[i, slot * rows : (slot + 1) * rows] = first_in[
                slot, pl.ds(i, rows, stride=rows)
            ]

    first_all = whole_first[...].reshape(rows * half, width)
    gate = jax.nn.sigmoid(
        jnp.dot(
            norm(first_all).astype(jnp.bfloat16),
            mult_gate_ref[...],
            preferred_element_type=jnp.float32,
        )
    )
    tri_normed = norm(tri[...].reshape(rows * half, width)).astype(jnp.bfloat16)
    second = first_all + gate * jnp.dot(
        tri_normed, mult_out_ref[...], preferred_element_type=jnp.float32
    )
    last_normed = norm(second).astype(jnp.bfloat16)
    hidden = jax.nn.relu(
        jnp.dot(last_normed, trans_up_ref[...], preferred_element_type=jnp.float32)
    ).astype(jnp.bfloat16)
    result = second + jnp.dot(hidden, trans_down_ref[...], preferred_element_type=jnp.float32)
    out_ref[...] = result.astype(jnp.bfloat16).reshape(rows, half, width)


def local(
    pair,
    length,
    chain,
    att_proj,
    att_bias,
    chain_bias,
    att_out,
    mult_in,
    mult_gate,
    mult_out,
    trans_up,
    trans_down,
):
    rows, cols, width = pair.shape
    n_row, n_col, n_sub = (lax.axis_size(a) for a in ("row", "col", "sub"))
    owners = n_col * n_sub
    slots = n_row // owners
    area = rows * rows
    half = cols // n_sub
    total = rows * n_row
    heads_here = att_bias.shape[1]
    heads = heads_here * n_sub
    spread = att_out.shape[0]
    vmem = pl.BlockSpec(memory_space=pltpu.VMEM)
    smem = pl.BlockSpec(memory_space=pltpu.SMEM)
    dma = pltpu.SemaphoreType.DMA
    bf16, f32 = jnp.bfloat16, jnp.float32
    return pl.pallas_call(
        functools.partial(pair_kernel, n_row, n_col, n_sub),
        out_shape=jax.ShapeDtypeStruct((rows, half, width), bf16),
        in_specs=[smem] * 3 + [vmem] * 10,
        out_specs=vmem,
        scratch_shapes=[
            pltpu.VMEM((n_col, rows, cols, width), bf16),
            pltpu.VMEM((rows // 2, cols, width), f32),
            pltpu.VMEM((slots, area, width), f32),
            pltpu.VMEM((rows, total, 2 * width), bf16),
            pltpu.VMEM((slots, area, width), f32),
            pltpu.VMEM((heads * half, width), f32),
            pltpu.VMEM((slots, area, width), f32),
            pltpu.VMEM((rows, heads * half, total), f32),
            pltpu.VMEM((heads * half, total), f32),
            pltpu.VMEM((n_row, heads_here * rows, width), f32),
            pltpu.VMEM((owners, slots, heads_here * rows, width), f32),
            pltpu.VMEM((n_sub, 4, spread, width), bf16),
            pltpu.VMEM((n_sub, spread, width), bf16),
            pltpu.VMEM((slots, area, width), f32),
            pltpu.VMEM((slots, area, width), f32),
            pltpu.VMEM((slots, area, width), f32),
            pltpu.VMEM((rows, half, width), f32),
            pltpu.VMEM((n_row, slots, area, width), bf16),
            pltpu.VMEM((slots, area, width), f32),
            pltpu.VMEM((area + 8, width), f32),
            pltpu.VMEM((n_row, area, width), f32),
            pltpu.VMEM((n_row, area, width), bf16),
            pltpu.VMEM((owners, slots, area, width), bf16),
            pltpu.VMEM((rows, half, width), f32),
            dma((2, 2, 2)),
            dma((2, 2, 2)),
            dma((2,)),
            dma((2,)),
            dma((n_row // STRIDE, 2)),
            dma((n_row,)),
            dma((n_row // STRIDE, STRIDE)),
            dma((owners, slots)),
            dma((slots,)),
            dma((slots,)),
            dma((2, 2, slots)),
            dma((2, n_row // 2, slots)),
            dma((n_row,)),
            dma((owners, slots)),
        ],
        compiler_params=pltpu.CompilerParams(collective_id=0, has_side_effects=True),
    )(
        length,
        chain,
        chain_bias,
        pair,
        chain,
        att_bias.T,
        att_proj.transpose(1, 2, 0),
        att_out,
        mult_in,
        mult_gate,
        mult_out,
        trans_up,
        trans_down,
    )


def solution(mesh):
    placed = (
        P(("grp", "row"), "col", None),
        P("grp"),
        P("grp"),
        P(None, None, "sub"),
        P(None, "sub"),
        P("sub"),
        P("sub", None),
        P(),
        P(),
        P(),
        P(),
        P(),
    )
    return jax.shard_map(
        local,
        mesh=mesh,
        in_specs=placed,
        out_specs=P(("grp", "row"), ("col", "sub"), None),
        check_vma=False,
    )
```

time: 145 us -> 176 us (1.21)
  Pallas kernels: 141 us -> 174 us
    pallas_call x1, Pallas kernels: 141 us -> 174 us  [local(): pl.pallas_call(functools.partial(pair_kernel, n_row, n_col, n_sub), out_s...]
where the time goes in v5:
time: 176 us
  Pallas kernels  174 us (99%)
    pallas_call x1, Pallas kernels, local(): pl.pallas_call(functools.partial(pair_kernel, n_row, n_col, n_sub), out_s...  174 us

profile of v5, /device:TPU:44, one launch (start us, length us, event | category | flops | bytes accessed | tf_op | source)
XLA Modules:
  0.0 176.1 jit_solution(2393583264367394244)
XLA Ops:
  0.7 173.9 %shard_map.118 = bf16[12,48,128]{2,1,0:T(8,128)(2,1)} custom-call(s32[1]{0:T(128)S(6)} %copy.14.length_ref, s32[384]{0:T(512)} %chain_lanes_ref.1, f32[2]{0:T(128)} %chain_bias_ref.1, bf16[12,96,128]{2,1,0:T(8,128)(2,1)} %pair_ref.1, s32[384]{0:T(512)} %chain_lanes_ref.1, bf16[2,128]{1,0:T(2,128)(2,1)} %bitcast.3, bf16[4,64,128]{2,1,0:T(8,128)(2,1)} %bitcast.2, ...), custom_call_target="tpu_custom_call" | custom-call | tf_op jit(solution)/shard_map/pallas_call | solution.py:675
  174.5 1.6 copy.15

commit v6 on v3

--- a/solution.py
+++ b/solution.py
@@ -59,6 +59,8 @@
     gate,
     x_send,
     x_recv,
+    swap_send,
+    swap_recv,
     weight_send,
     weight_recv,
     chain_send,
@@ -117,7 +119,7 @@
     key = begin + lax.rem(lane + (width - turn), width)
     key_chain = jnp.zeros((1, width), jnp.int32)
     for k in range(total // width):
-        held = chain_lanes_ref[:, k * width : (k + 1) * width]
+        held = chain_lanes_ref[k * width : (k + 1) * width].reshape(1, width)
         key_chain = jnp.where(key // width == k, held, key_chain)
     key_bias = ((key < length).astype(jnp.float32) - 1.0) * 1000000000.0
     padding = jnp.zeros((width - cols, width), jnp.bfloat16)
@@ -149,16 +151,35 @@
             device_id_type=MESH,
         )
 
-    def x_copy(way, step, chunk, arrives):
+    quarter = block_rows // 2
+    x_up = lax.rem(x + n_col - 1, n_col)
+    x_down = lax.rem(x + 1, n_col)
+    x_far = lax.rem(x + 2, n_col)
+
+    def x_copy(way, step, arrives):
         distance = step + 1 if arrives else step
         source = lax.rem(x + (n_col - distance if way == 0 else distance), n_col)
-        block = normed.at[source, pl.ds(chunk * block_rows, block_rows)]
+        begin_row = core * block_rows + (quarter if step == 1 and way == 1 else 0)
+        block = normed.at[source, pl.ds(begin_row, block_rows if step == 0 else quarter)]
         return pltpu.make_async_remote_copy(
             src_ref=block,
             dst_ref=block,
-            send_sem=x_send.at[way, step, chunk],
-            recv_sem=x_recv.at[way, step, chunk],
+            send_sem=x_send.at[way, step],
+            recv_sem=x_recv.at[way, step],
             device_id={"col": lax.rem(x + (1 if way == 0 else n_col - 1), n_col)},
+            device_id_type=MESH,
+        )
+
+    def swap(k, holder):
+        source = (x_up, x_down, x_far, x_far)[k]
+        begin_row = holder * block_rows + (quarter if k == 3 else 0)
+        block = normed.at[source, pl.ds(begin_row, block_rows if k < 2 else quarter)]
+        return pltpu.make_async_remote_copy(
+            src_ref=block,
+            dst_ref=block,
+            send_sem=swap_send.at[k],
+            recv_sem=swap_recv.at[k],
+            device_id={"sub": 1 - core},
             device_id_type=MESH,
         )
 
@@ -245,13 +266,11 @@
         )
         return carry
 
+    for way in range(2):
+        x_copy(way, 0, False).start()
     pass_on(0)
     for k in range(2):
         weight_copy(k).start()
-    for chunk in range(2):
-        for way in range(2):
-            x_copy(way, 0, chunk if way == 0 else 1 - chunk, False).start()
-
     for k in range(2):
         weight_copy(k).wait_recv()
 
@@ -276,10 +295,6 @@
     for chunk in range(2):
         project(x, chunk)
 
-    x_up = lax.rem(x + n_col - 1, n_col)
-    x_down = lax.rem(x + 1, n_col)
-    x_far = lax.rem(x + 2, n_col)
-
     def stage_of(step):
         if step <= ups:
             pass_on(step)
@@ -289,25 +304,28 @@
         if 1 <= step - 1 < ups:
             take_local(ups + step - 1)
 
+    for way in range(2):
+        x_copy(way, 0, True).wait_recv()
+        x_copy(way, 1, False).start()
+        swap(way, core).start()
     stage_of(1)
-    x_copy(0, 0, 0, True).wait_recv()
-    x_copy(0, 1, 0, False).start()
-    x_copy(1, 0, 1, True).wait_recv()
-    x_copy(1, 1, 1, False).start()
-    project(x_up, 0)
-    project(x_down, 1)
+    project(x_up, core)
+    project(x_down, core)
+    for way in range(2):
+        x_copy(way, 1, True).wait_recv()
+        swap(2 + way, core).start()
     stage_of(2)
-    x_copy(0, 0, 1, True).wait_recv()
-    project(x_up, 1)
-    x_copy(1, 0, 0, True).wait_recv()
-    project(x_down, 0)
+    project(x_far, core)
+    swap(0, 1 - core).wait_recv()
+    project(x_up, 1 - core)
+    swap(1, 1 - core).wait_recv()
+    project(x_down, 1 - core)
     stage_of(3)
-    x_copy(0, 1, 0, True).wait_recv()
-    project(x_far, 0)
+    swap(2, 1 - core).wait_recv()
+    swap(3, 1 - core).wait_recv()
+    project(x_far, 1 - core)
     lax.fori_loop(0, block_rows, score, 0)
     stage_of(4)
-    x_copy(1, 1, 1, True).wait_recv()
-    project(x_far, 1)
     lax.fori_loop(block_rows, rows, score, 0)
     take_local(ups)
 
@@ -460,9 +478,10 @@
     for k in range(2):
         weight_copy(k).wait_send()
     for way in range(2):
-        for chunk in range(2):
-            x_copy(way, 0, chunk, False).wait_send()
-        x_copy(way, 1, way, False).wait_send()
+        for step in range(2):
+            x_copy(way, step, False).wait_send()
+    for k in range(4):
+        swap(k, core).wait_send()
 
     def sent(block, carry):
         @pl.when(lax.div(block, per_owner) != me)
@@ -549,8 +568,10 @@
             pltpu.VMEM((owners, per_owner, rows * rows, width), bf16),
             pltpu.VMEM((rows, half, width), f32),
             pltpu.VMEM((rows * half, width), f32),
-            dma((2, 2, 2)),
-            dma((2, 2, 2)),
+            dma((2, 2)),
+            dma((2, 2)),
+            dma((4,)),
+            dma((4,)),
             dma((2,)),
             dma((2,)),
             dma((n_row // STRIDE, len(LOCAL) + 2)),
@@ -568,7 +589,7 @@
         chain,
         chain_bias,
         pair,
-        chain[None],
+        chain,
         att_bias.T,
         att_proj.transpose(1, 2, 0),
         att_out,

time: 145 us -> 144 us (level)
  no operation moved by 1% of the time
where the time goes in v6:
time: 144 us; the launch traced here: 143 us
  Pallas kernels  141 us (98%)
  local copies, waits for them, and re-layouts  1.58 us (1%)
    pallas_call x1, Pallas kernels, local(): pl.pallas_call(functools.partial(pair_kernel, n_row, n_col, n_sub), out_s...  141 us

profile of v6, /device:TPU:44, one launch (start us, length us, event | category | flops | bytes accessed | tf_op | source)
XLA Modules:
  0.0 143.4 jit_solution(17789987373499963366)
XLA Ops:
  0.7 141.2 %shard_map.118 = bf16[12,48,128]{2,1,0:T(8,128)(2,1)} custom-call(s32[1]{0:T(128)S(6)} %copy.14.length_ref, s32[384]{0:T(512)} %chain_lanes_ref.1, f32[2]{0:T(128)} %chain_bias_ref.1, bf16[12,96,128]{2,1,0:T(8,128)(2,1)} %pair_ref.1, s32[384]{0:T(512)} %chain_lanes_ref.1, bf16[2,128]{1,0:T(2,128)(2,1)} %bitcast.3, bf16[4,64,128]{2,1,0:T(8,128)(2,1)} %bitcast.2, ...), custom_call_target="tpu_custom_call" | custom-call | tf_op jit(solution)/shard_map/pallas_call | solution.py:546
  141.8 1.6 %copy.15 = bf16[12,48,128]{2,1,0:T(8,128)(2,1)} copy(bf16[12,48,128]{2,1,0:T(8,128)(2,1)} %shard_map.118) | data formatting | bytes 294912

commit v7 on v6

--- a/solution.py
+++ b/solution.py
@@ -296,13 +296,12 @@
         project(x, chunk)
 
     def stage_of(step):
-        if step <= ups:
-            pass_on(step)
+        take_local(step - 1)
+        if step > 1:
+            take_local(ups + step - 1)
+        pass_on(step)
         if step < ups:
             pass_on(ups + step)
-        take_local(step - 1)
-        if 1 <= step - 1 < ups:
-            take_local(ups + step - 1)
 
     for way in range(2):
         x_copy(way, 0, True).wait_recv()

time: 144 us -> 145 us (level)
  no operation moved by 1% of the time
where the time goes in v7:
time: 145 us; the launch traced here: 144 us
  Pallas kernels  142 us (98%)
  local copies, waits for them, and re-layouts  1.58 us (1%)
    pallas_call x1, Pallas kernels, local(): pl.pallas_call(functools.partial(pair_kernel, n_row, n_col, n_sub), out_s...  142 us

profile of v7, /device:TPU:44, one launch (start us, length us, event | category | flops | bytes accessed | tf_op | source)
XLA Modules:
  0.0 144.5 jit_solution(3879438928255600070)
XLA Ops:
  0.7 142.2 %shard_map.118 = bf16[12,48,128]{2,1,0:T(8,128)(2,1)} custom-call(s32[1]{0:T(128)S(6)} %copy.14.length_ref, s32[384]{0:T(512)} %chain_lanes_ref.1, f32[2]{0:T(128)} %chain_bias_ref.1, bf16[12,96,128]{2,1,0:T(8,128)(2,1)} %pair_ref.1, s32[384]{0:T(512)} %chain_lanes_ref.1, bf16[2,128]{1,0:T(2,128)(2,1)} %bitcast.3, bf16[4,64,128]{2,1,0:T(8,128)(2,1)} %bitcast.2, ...), custom_call_target="tpu_custom_call" | custom-call | tf_op jit(solution)/shard_map/pallas_call | solution.py:545
  142.9 1.6 %copy.15 = bf16[12,48,128]{2,1,0:T(8,128)(2,1)} copy(bf16[12,48,128]{2,1,0:T(8,128)(2,1)} %shard_map.118) | data formatting | bytes 294912
